TPU v7x, 8 devices: a whole 2x2x1 slice. The times are simulated.
8 devices in a mesh: dp: 1 (over z), tp: 2 (over y), cp: 4 (over x, core).
Axes of the slice: x: 2, y: 2, z: 1, core: 2. Of those that a mesh axis runs over, the one named last changes fastest.
Arguments:
- x: bfloat16 [4096, 6144], P(('dp', 'cp'))
- k_cache: bfloat16 [1024, 8, 128], P(('dp', 'cp'), 'tp')
- v_cache: bfloat16 [1024, 8, 128], P(('dp', 'cp'), 'tp')
- rope_table: float32 [4096, 64], P(('dp', 'cp'))
- norm_gain: bfloat16 [6144], replicated
- w_qkv: bfloat16 [6144, 8192], P(None, 'tp')
- b_qkv: bfloat16 [8192], P('tp')
- w_out: bfloat16 [6144, 6144], P('tp')
Outputs:
- output 1: bfloat16 [4096, 6144], P(('dp', 'cp'))
- output 2: bfloat16 [4096, 8, 128], P(('dp', 'cp'), 'tp')
- output 3: bfloat16 [4096, 8, 128], P(('dp', 'cp'), 'tp')
All inputs are finite; a program needn't handle non-finite values.
Results may differ from a plain program's by a relative error of at most 0.0044295.
Values are sent between devices in bfloat16 or wider.
A program may use at most 1 GiB of HBM per device.

v0:
```python
import jax
import jax.numpy as jnp
from jax import lax
from jax.sharding import PartitionSpec as P, NamedSharding

EPS = 1.5625e-07
MASK_VALUE = -1e30


def apply_rotary(vals, cos_t, sin_t):
    pair_count = cos_t.shape[-1]
    lead_shape = vals.shape[:-1]
    paired = vals[..., :2 * pair_count].reshape(lead_shape + (pair_count, 2))
    even_part = paired[..., 0]
    odd_part = paired[..., 1]
    turned = jnp.stack([even_part * cos_t - odd_part * sin_t, odd_part * cos_t + even_part * sin_t], axis=-1)
    return jnp.concatenate([turned.reshape(lead_shape + (2 * pair_count,)), vals[..., 2 * pair_count:]], axis=-1)


def project_new(x, rope_table, norm_gain, w_qkv, b_qkv, kv_count, head_dim):
    x_f32 = x.astype(jnp.float32)
    inv_rms = lax.rsqrt(jnp.mean(x_f32 * x_f32, axis=-1, keepdims=True) + EPS)
    hidden = (x_f32 * inv_rms * norm_gain.astype(jnp.float32)).astype(jnp.bfloat16)
    tok_rows = x.shape[0]
    group = w_qkv.shape[1] // (kv_count * head_dim) - 2
    qkv_all = jnp.dot(hidden, w_qkv, preferred_element_type=jnp.float32) + b_qkv.astype(jnp.float32)
    qkv_all = qkv_all.reshape(tok_rows, kv_count, group + 2, head_dim)
    pair_count = rope_table.shape[1] // 2
    cos_t = rope_table[:, :pair_count]
    sin_t = rope_table[:, pair_count:]
    queries = apply_rotary(qkv_all[:, :, :group], cos_t[:, None, None], sin_t[:, None, None]).astype(jnp.bfloat16)
    new_k = apply_rotary(qkv_all[:, :, group], cos_t[:, None], sin_t[:, None]).astype(jnp.bfloat16)
    new_v = qkv_all[:, :, group + 1].astype(jnp.bfloat16)
    return x_f32, queries, new_k, new_v


def local_step(x, k_cache, v_cache, rope_table, norm_gain, w_qkv, b_qkv, w_out):
    kv_local, head_dim = k_cache.shape[1], k_cache.shape[2]
    tok_rows = x.shape[0]
    x_f32, queries, new_k, new_v = project_new(x, rope_table, norm_gain, w_qkv, b_qkv, kv_local, head_dim)
    group = queries.shape[2]
    k_prefix = lax.all_gather(k_cache, 'cp')
    v_prefix = lax.all_gather(v_cache, 'cp')
    k_recent = lax.all_gather(new_k, 'cp')
    v_recent = lax.all_gather(new_v, 'cp')
    cp_size = k_prefix.shape[0]
    scale = head_dim ** -0.5
    q_pos = lax.axis_index('cp') * tok_rows + jnp.arange(tok_rows)

    def attend(carry, block):
        run_max, run_sum, weighted = carry
        kp_block, vp_block, kr_block, vr_block, source = block
        s_pref = jnp.einsum('tngd,knd->tngk', queries, kp_block, preferred_element_type=jnp.float32) * scale
        s_recent = jnp.einsum('tngd,knd->tngk', queries, kr_block, preferred_element_type=jnp.float32) * scale
        k_pos = source * tok_rows + jnp.arange(tok_rows)
        visible = (k_pos[None, :] <= q_pos[:, None])[:, None, None, :]
        s_recent = jnp.where(visible, s_recent, MASK_VALUE)
        new_max = jnp.maximum(run_max, jnp.maximum(s_pref.max(axis=-1), s_recent.max(axis=-1)))
        rescale = jnp.exp(run_max - new_max)
        p_pref = jnp.exp(s_pref - new_max[..., None])
        p_recent = jnp.exp(s_recent - new_max[..., None])
        run_sum = run_sum * rescale + p_pref.sum(axis=-1) + p_recent.sum(axis=-1)
        weighted = (weighted * rescale[..., None]
                    + jnp.einsum('tngk,knd->tngd', p_pref.astype(jnp.bfloat16), vp_block, preferred_element_type=jnp.float32)
                    + jnp.einsum('tngk,knd->tngd', p_recent.astype(jnp.bfloat16), vr_block, preferred_element_type=jnp.float32))
        return (new_max, run_sum, weighted), None

    stat_shape = (tok_rows, kv_local, group)
    start_carry = (jnp.full(stat_shape, MASK_VALUE, jnp.float32), jnp.zeros(stat_shape, jnp.float32), jnp.zeros(stat_shape + (head_dim,), jnp.float32))
    (run_max, run_sum, weighted), _ = lax.scan(attend, start_carry, (k_prefix, v_prefix, k_recent, v_recent, jnp.arange(cp_size)))
    attn = (weighted / run_sum[..., None]).astype(jnp.bfloat16).reshape(tok_rows, kv_local * group * head_dim)
    proj_part = jnp.dot(attn, w_out, preferred_element_type=jnp.float32)
    y = (x_f32 + lax.psum(proj_part, 'tp')).astype(jnp.bfloat16)
    return y, new_k, new_v


def solution(mesh):
    row_spec = P(('dp', 'cp'), None)
    cache_spec = P(('dp', 'cp'), 'tp', None)
    return jax.shard_map(local_step, mesh=mesh, in_specs=(row_spec, cache_spec, cache_spec, row_spec, P(None), P(None, 'tp'), P('tp'), P('tp', None)), out_specs=(row_spec, cache_spec, cache_spec), check_vma=False)
```

profile of v0, /device:TPU:0, one launch (start us, length us, event | category | flops | bytes accessed | tf_op | source)
XLA Modules:
  0.0 1463.6 jit_solution(12110263377779714384)
XLA Ops:
  17.9 61.4 %add_bitcast_fusion = f32[128,8,32,128]{3,1,2,0:T(8,128)} fusion(bf16[6144,4096]{1,0:T(8,128)(2,1)} %param.15, bf16[1024,6144]{1,0:T(8,128)(2,1)} %param.10, f32[6144]{0:T(1024)S(1)} %convert_element_type.50, f32[1024]{0:T(1024)S(1)} %add_rsqrt_fusion, f32[4096]{0:T(1024)S(1)} %convert_element_type.52), kind=kOutput, calls=%fused_computation.50 | convolution fusion | flops 51568967680 | bytes 79736832 | tf_op jit(solution)/shard_map/dot_general | solution.py:26
  120.3 12.9 copy.62
  133.2 11.4 copy.63
  159.1 11.2 copy.48
  170.3 657.7 %while.15 = (s32[]{:T(128)}, f32[1024,4,6]{0,2,1:T(8,128)S(1)}, f32[1024,4,6]{0,2,1:T(8,128)S(1)}, f32[1024,4,6,128]{0,3,2,1:T(8,128)}, bf16[4,256,4,128]{3,1,0,...) while((s32[]{:T(128)}, f32[1024,4,6]{0,2,1:T(8,128)S(1)}, ...), condition=%wide.region_6.7_spmd.clone, body=%wide.region_1.6_spmd.clone.sunk | while | flops 16447039488 | bytes 453591232 | solution.py:70
  186.3 14.7 %bitcast_reduce_fusion.2 = (f32[1024,4,6]{0,2,1:T(8,128)S(1)}, f32[4,256,1024,6]{2,1,3,0:T(8,128)}) fusion(bf16[1024,4,6,128]{3,0,2,1:T(8,128)(2,1)} %get-tuple-element.295, bf16[4,256,4,128]{3,1,0,2:T(8,128)(2,1)} %get-tuple-element.294, s32[]{:T(128)S(6)} %copy.72), kind=kOutput, calls=%fused_computation.9.clone.1 | convolution fusion | flops 1623171072 | bytes 31817732 | tf_op jit(solution)/shard_map/while/body/eval_jaxpr/tngd,knd->tngk/dot_general | solution.py:53
  201.0 37.6 %fusion.72 = (f32[1024,4,6]{0,2,1:T(8,128)S(1)}, f32[4,1024,1024,6]{2,1,3,0:T(8,128)}) fusion(pred[1024,1024]{0,1:T(8,128)(4,1)S(1)} %broadcast_compare_fusion.2, bf16[1024,4,6,128]{3,0,2,1:T(8,128)(2,1)} %get-tuple-element.295, bf16[4,1024,4,128]{3,1,2,0:T(8,128)(2,1)} %get-tuple-element.297, s32[]{:T(128)S(6)} %copy.72), kind=kOutput, calls=%fused_computation.5.clone.1 | convolution fusion | flops 6517923840 | bytes 109150208 | tf_op jit(solution)/shard_map/while/body/eval_jaxpr/tngd,knd->tngk/dot_general | solution.py:54
  238.6 10.5 fusion.74
  249.1 31.3 %fusion.73 = f32[1024,4,6]{0,2,1:T(8,128)S(1)} fusion(f32[4,1024,1024,6]{2,1,3,0:T(8,128)} %get-tuple-element.258, f32[1024,4,6]{0,2,1:T(8,128)S(1)} %maximum_maximum_fusion.2, pred[1024,1024]{0,1:T(8,128)(4,1)S(1)} %broadcast_compare_fusion.2), kind=kLoop, calls=%fused_computation.4.clone.1 | loop fusion | flops 100638720 | bytes 101908480 | tf_op jit(solution)/shard_map/while/body/eval_jaxpr/reduce_sum | solution.py:62
  280.4 41.3 %fusion.76 = f32[4,128,1024,6]{2,1,3,0:T(8,128)} fusion(f32[4,1024,1024,6]{2,1,3,0:T(8,128)} %get-tuple-element.258, f32[1024,4,6]{0,2,1:T(8,128)S(1)} %maximum_maximum_fusion.2, pred[1024,1024]{0,1:T(8,128)(4,1)S(1)} %broadcast_compare_fusion.2, bf16[1,1024,4,128]{1,3,2,0:T(8,128)(2,1)S(1)} %copy.67), kind=kOutput, calls=%fused_computation.6.clone.1 | convolution fusion | flops 6543114240 | bytes 115441664 | tf_op jit(solution)/shard_map/while/body/eval_jaxpr/tngk,knd->tngd/dot_general | solution.py:65
  321.8 19.0 %bitcast_add_fusion.3 = f32[1024,4,6,128]{0,3,2,1:T(8,128)} fusion(f32[4,128,1024,6]{2,1,3,0:T(8,128)} %fusion.76, f32[1024,4,6,128]{0,3,2,1:T(8,128)} %get-tuple-element.279, f32[1024,4,6]{0,2,1:T(8,128)S(1)} %get-tuple-element.261, pred[]{:T(512)S(6)} %compare.3, f32[4,256,1024,6]{2,1,3,0:T(8,128)} %get-tuple-element.259, ...), kind=kOutput, calls=%fused_computation.14.clone.1 | convolution fusion | flops 1642070016 | bytes 63373316 | tf_op jit(solution)/shard_map/while/body/eval_jaxpr/tngk,knd->tngd/dot_general | solution.py:64
  345.1 14.7 %bitcast_reduce_fusion.2 = (f32[1024,4,6]{0,2,1:T(8,128)S(1)}, f32[4,256,1024,6]{2,1,3,0:T(8,128)}) fusion(bf16[1024,4,6,128]{3,0,2,1:T(8,128)(2,1)} %get-tuple-element.295, bf16[4,256,4,128]{3,1,0,2:T(8,128)(2,1)} %get-tuple-element.294, s32[]{:T(128)S(6)} %copy.72), kind=kOutput, calls=%fused_computation.9.clone.1 | convolution fusion | flops 1623171072 | bytes 31817732 | tf_op jit(solution)/shard_map/while/body/eval_jaxpr/tngd,knd->tngk/dot_general | solution.py:53
  359.7 37.6 %fusion.72 = (f32[1024,4,6]{0,2,1:T(8,128)S(1)}, f32[4,1024,1024,6]{2,1,3,0:T(8,128)}) fusion(pred[1024,1024]{0,1:T(8,128)(4,1)S(1)} %broadcast_compare_fusion.2, bf16[1024,4,6,128]{3,0,2,1:T(8,128)(2,1)} %get-tuple-element.295, bf16[4,1024,4,128]{3,1,2,0:T(8,128)(2,1)} %get-tuple-element.297, s32[]{:T(128)S(6)} %copy.72), kind=kOutput, calls=%fused_computation.5.clone.1 | convolution fusion | flops 6517923840 | bytes 109150208 | tf_op jit(solution)/shard_map/while/body/eval_jaxpr/tngd,knd->tngk/dot_general | solution.py:54
  397.4 10.5 fusion.74
  407.9 31.3 %fusion.73 = f32[1024,4,6]{0,2,1:T(8,128)S(1)} fusion(f32[4,1024,1024,6]{2,1,3,0:T(8,128)} %get-tuple-element.258, f32[1024,4,6]{0,2,1:T(8,128)S(1)} %maximum_maximum_fusion.2, pred[1024,1024]{0,1:T(8,128)(4,1)S(1)} %broadcast_compare_fusion.2), kind=kLoop, calls=%fused_computation.4.clone.1 | loop fusion | flops 100638720 | bytes 101908480 | tf_op jit(solution)/shard_map/while/body/eval_jaxpr/reduce_sum | solution.py:62
  439.2 41.3 %fusion.76 = f32[4,128,1024,6]{2,1,3,0:T(8,128)} fusion(f32[4,1024,1024,6]{2,1,3,0:T(8,128)} %get-tuple-element.258, f32[1024,4,6]{0,2,1:T(8,128)S(1)} %maximum_maximum_fusion.2, pred[1024,1024]{0,1:T(8,128)(4,1)S(1)} %broadcast_compare_fusion.2, bf16[1,1024,4,128]{1,3,2,0:T(8,128)(2,1)S(1)} %copy.67), kind=kOutput, calls=%fused_computation.6.clone.1 | convolution fusion | flops 6543114240 | bytes 115441664 | tf_op jit(solution)/shard_map/while/body/eval_jaxpr/tngk,knd->tngd/dot_general | solution.py:65
  480.5 22.6 %bitcast_add_fusion.3 = f32[1024,4,6,128]{0,3,2,1:T(8,128)} fusion(f32[4,128,1024,6]{2,1,3,0:T(8,128)} %fusion.76, f32[1024,4,6,128]{0,3,2,1:T(8,128)} %get-tuple-element.279, f32[1024,4,6]{0,2,1:T(8,128)S(1)} %get-tuple-element.261, pred[]{:T(512)S(6)} %compare.3, f32[4,256,1024,6]{2,1,3,0:T(8,128)} %get-tuple-element.259, ...), kind=kOutput, calls=%fused_computation.14.clone.1 | convolution fusion | flops 1642070016 | bytes 63373316 | tf_op jit(solution)/shard_map/while/body/eval_jaxpr/tngk,knd->tngd/dot_general | solution.py:64
  507.4 14.7 %bitcast_reduce_fusion.2 = (f32[1024,4,6]{0,2,1:T(8,128)S(1)}, f32[4,256,1024,6]{2,1,3,0:T(8,128)}) fusion(bf16[1024,4,6,128]{3,0,2,1:T(8,128)(2,1)} %get-tuple-element.295, bf16[4,256,4,128]{3,1,0,2:T(8,128)(2,1)} %get-tuple-element.294, s32[]{:T(128)S(6)} %copy.72), kind=kOutput, calls=%fused_computation.9.clone.1 | convolution fusion | flops 1623171072 | bytes 31817732 | tf_op jit(solution)/shard_map/while/body/eval_jaxpr/tngd,knd->tngk/dot_general | solution.py:53
  522.1 37.6 %fusion.72 = (f32[1024,4,6]{0,2,1:T(8,128)S(1)}, f32[4,1024,1024,6]{2,1,3,0:T(8,128)}) fusion(pred[1024,1024]{0,1:T(8,128)(4,1)S(1)} %broadcast_compare_fusion.2, bf16[1024,4,6,128]{3,0,2,1:T(8,128)(2,1)} %get-tuple-element.295, bf16[4,1024,4,128]{3,1,2,0:T(8,128)(2,1)} %get-tuple-element.297, s32[]{:T(128)S(6)} %copy.72), kind=kOutput, calls=%fused_computation.5.clone.1 | convolution fusion | flops 6517923840 | bytes 109150208 | tf_op jit(solution)/shard_map/while/body/eval_jaxpr/tngd,knd->tngk/dot_general | solution.py:54
  559.7 10.5 fusion.74
  570.2 31.3 %fusion.73 = f32[1024,4,6]{0,2,1:T(8,128)S(1)} fusion(f32[4,1024,1024,6]{2,1,3,0:T(8,128)} %get-tuple-element.258, f32[1024,4,6]{0,2,1:T(8,128)S(1)} %maximum_maximum_fusion.2, pred[1024,1024]{0,1:T(8,128)(4,1)S(1)} %broadcast_compare_fusion.2), kind=kLoop, calls=%fused_computation.4.clone.1 | loop fusion | flops 100638720 | bytes 101908480 | tf_op jit(solution)/shard_map/while/body/eval_jaxpr/reduce_sum | solution.py:62
  601.5 41.3 %fusion.76 = f32[4,128,1024,6]{2,1,3,0:T(8,128)} fusion(f32[4,1024,1024,6]{2,1,3,0:T(8,128)} %get-tuple-element.258, f32[1024,4,6]{0,2,1:T(8,128)S(1)} %maximum_maximum_fusion.2, pred[1024,1024]{0,1:T(8,128)(4,1)S(1)} %broadcast_compare_fusion.2, bf16[1,1024,4,128]{1,3,2,0:T(8,128)(2,1)S(1)} %copy.67), kind=kOutput, calls=%fused_computation.6.clone.1 | convolution fusion | flops 6543114240 | bytes 115441664 | tf_op jit(solution)/shard_map/while/body/eval_jaxpr/tngk,knd->tngd/dot_general | solution.py:65
  642.9 22.6 %bitcast_add_fusion.3 = f32[1024,4,6,128]{0,3,2,1:T(8,128)} fusion(f32[4,128,1024,6]{2,1,3,0:T(8,128)} %fusion.76, f32[1024,4,6,128]{0,3,2,1:T(8,128)} %get-tuple-element.279, f32[1024,4,6]{0,2,1:T(8,128)S(1)} %get-tuple-element.261, pred[]{:T(512)S(6)} %compare.3, f32[4,256,1024,6]{2,1,3,0:T(8,128)} %get-tuple-element.259, ...), kind=kOutput, calls=%fused_computation.14.clone.1 | convolution fusion | flops 1642070016 | bytes 63373316 | tf_op jit(solution)/shard_map/while/body/eval_jaxpr/tngk,knd->tngd/dot_general | solution.py:64
  669.7 14.7 %bitcast_reduce_fusion.2 = (f32[1024,4,6]{0,2,1:T(8,128)S(1)}, f32[4,256,1024,6]{2,1,3,0:T(8,128)}) fusion(bf16[1024,4,6,128]{3,0,2,1:T(8,128)(2,1)} %get-tuple-element.295, bf16[4,256,4,128]{3,1,0,2:T(8,128)(2,1)} %get-tuple-element.294, s32[]{:T(128)S(6)} %copy.72), kind=kOutput, calls=%fused_computation.9.clone.1 | convolution fusion | flops 1623171072 | bytes 31817732 | tf_op jit(solution)/shard_map/while/body/eval_jaxpr/tngd,knd->tngk/dot_general | solution.py:53
  684.4 37.6 %fusion.72 = (f32[1024,4,6]{0,2,1:T(8,128)S(1)}, f32[4,1024,1024,6]{2,1,3,0:T(8,128)}) fusion(pred[1024,1024]{0,1:T(8,128)(4,1)S(1)} %broadcast_compare_fusion.2, bf16[1024,4,6,128]{3,0,2,1:T(8,128)(2,1)} %get-tuple-element.295, bf16[4,1024,4,128]{3,1,2,0:T(8,128)(2,1)} %get-tuple-element.297, s32[]{:T(128)S(6)} %copy.72), kind=kOutput, calls=%fused_computation.5.clone.1 | convolution fusion | flops 6517923840 | bytes 109150208 | tf_op jit(solution)/shard_map/while/body/eval_jaxpr/tngd,knd->tngk/dot_general | solution.py:54
  722.0 10.5 fusion.74
  732.5 31.3 %fusion.73 = f32[1024,4,6]{0,2,1:T(8,128)S(1)} fusion(f32[4,1024,1024,6]{2,1,3,0:T(8,128)} %get-tuple-element.258, f32[1024,4,6]{0,2,1:T(8,128)S(1)} %maximum_maximum_fusion.2, pred[1024,1024]{0,1:T(8,128)(4,1)S(1)} %broadcast_compare_fusion.2), kind=kLoop, calls=%fused_computation.4.clone.1 | loop fusion | flops 100638720 | bytes 101908480 | tf_op jit(solution)/shard_map/while/body/eval_jaxpr/reduce_sum | solution.py:62
  763.8 41.3 %fusion.76 = f32[4,128,1024,6]{2,1,3,0:T(8,128)} fusion(f32[4,1024,1024,6]{2,1,3,0:T(8,128)} %get-tuple-element.258, f32[1024,4,6]{0,2,1:T(8,128)S(1)} %maximum_maximum_fusion.2, pred[1024,1024]{0,1:T(8,128)(4,1)S(1)} %broadcast_compare_fusion.2, bf16[1,1024,4,128]{1,3,2,0:T(8,128)(2,1)S(1)} %copy.67), kind=kOutput, calls=%fused_computation.6.clone.1 | convolution fusion | flops 6543114240 | bytes 115441664 | tf_op jit(solution)/shard_map/while/body/eval_jaxpr/tngk,knd->tngd/dot_general | solution.py:65
  805.2 22.6 %bitcast_add_fusion.3 = f32[1024,4,6,128]{0,3,2,1:T(8,128)} fusion(f32[4,128,1024,6]{2,1,3,0:T(8,128)} %fusion.76, f32[1024,4,6,128]{0,3,2,1:T(8,128)} %get-tuple-element.279, f32[1024,4,6]{0,2,1:T(8,128)S(1)} %get-tuple-element.261, pred[]{:T(512)S(6)} %compare.3, f32[4,256,1024,6]{2,1,3,0:T(8,128)} %get-tuple-element.259, ...), kind=kOutput, calls=%fused_computation.14.clone.1 | convolution fusion | flops 1642070016 | bytes 63373316 | tf_op jit(solution)/shard_map/while/body/eval_jaxpr/tngk,knd->tngd/dot_general | solution.py:64
  837.4 47.2 %fusion.46 = f32[1024,6144]{1,0:T(8,128)} fusion(bf16[1024,3072]{0,1:T(8,128)(2,1)} %bitcast.127, bf16[3072,6144]{1,0:T(8,128)(2,1)} %param.17), kind=kOutput, calls=%fused_computation.69 | convolution fusion | flops 38654705664 | bytes 69206016 | tf_op jit(solution)/shard_map/dot_general | solution.py:72
  892.7 546.9 %all-reduce.2.cloned.1.call-done = f32[1024,6144]{1,0:T(8,128)} async-done(((f32[1024,6144]{1,0:T(8,128)}), f32[1024,6144]{1,0:T(8,128)}) %all-reduce.2.cloned.1.call-update) | async-done | bytes 25165840 | tf_op jit(solution)/shard_map/psum | solution.py:73
  1439.6 17.1 %fusion.37 = bf16[1024,6144]{1,0:T(8,128)(2,1)} fusion(f32[1024,6144]{1,0:T(8,128)} %all-reduce.2.cloned.1.call-done, bf16[1024,6144]{1,0:T(8,128)(2,1)} %param.10), kind=kLoop, calls=%fused_computation.49 | loop fusion | flops 18874368 | bytes 50331648 | tf_op jit(solution)/shard_map/convert_element_type | solution.py:73
  (98 shorter events, 97.8 us)
Async XLA Ops:
  7.2 10.7 copy-start.10
  7.2 10.7 copy-start.9
  7.2 163.1 %all-gather.10.cloned.1.call-start = ((), (), s32[]{:S(2)}) async-start(), calls=%async_computation.2 | async-start | bytes 1310720 | tf_op jit(solution)/shard_map/all_gather | solution.py:42
  9.0 161.3 %all-gather.12.cloned.1.call-start = ((), (), s32[]{:S(2)}) async-start(), calls=%async_computation.3 | async-start | bytes 1310720 | tf_op jit(solution)/shard_map/all_gather | solution.py:43
  10.7 159.6 %all-gather.14.cloned.1.call-start = ((), (), s32[]{:S(2)}) async-start(), calls=%async_computation.4 | async-start | bytes 5242880 | tf_op jit(solution)/shard_map/all_gather | solution.py:45
  88.8 5.7 copy-start
  88.8 17.7 %copy-start.8 = (f32[1024,64]{0,1:T(8,128)S(1)}, f32[1024,64]{0,1:T(8,128)}, u32[]{:S(2)}) copy-start(f32[1024,64]{0,1:T(8,128)} %param.13) | copy-start | bytes 786436
  98.6 1.3 copy-start.1
  101.3 69.0 %all-gather.8.cloned.1.call-start = ((), (), s32[]{:S(2)}) async-start(), calls=%async_computation | async-start | bytes 5242880 | tf_op jit(solution)/shard_map/all_gather | solution.py:44
  106.4 13.9 copy-start.3
  106.5 1.1 copy-start.6
  107.2 0.8 copy-start.4
  110.5 1329.1 %all-reduce.2.cloned.1.call-start = ((), (), s32[]{:S(2)}) async-start(), calls=%async_computation.1 | async-start | bytes 50331648 | tf_op jit(solution)/shard_map/psum | solution.py:73
  120.3 24.4 %copy-start.7 = (f32[1024,32]{0,1:T(8,128)S(1)}, f32[1024,32]{0,1:T(8,128)}, u32[]{:S(2)}) copy-start(f32[1024,32]{0,1:T(8,128)} %copy-done.6) | copy-start | bytes 393220
  884.6 1.6 copy-start.5
  884.6 6.8 copy-start.2
Sparse Core Ops, SparseCore 0:
  9.5 16.5 all-gather.9
  27.6 13.7 all-gather.11
  101.4 34.3 all-gather.13
  137.7 31.5 all-gather.7
  884.8 554.7 all-reduce.1
where the time goes:
time: 1470 us; the launch traced here: 1460 us
  matrix products  570 us (39%)
  waiting for transfers between devices  547 us (37%)
  other arithmetic  224 us (15%)
  local copies, waits for them, and re-layouts  93.3 us (6%)
  loops' own time  14.9 us (1%)
    psum x1, waiting for transfers between devices, local_step(): y = (x_f32 + lax.psum(proj_part, 'tp')).astype(jnp.bfloat16)  547 us
    reduce_sum x8, other arithmetic, attend(): run_sum = run_sum * rescale + p_pref.sum(axis=-1) + p_recent.sum(axis=-1)  167 us
    dot_general x4, matrix products, attend(): jnp.einsum('tngk,knd->tngd', p_recent.astype(jnp.bfloat16), vr_block, pre...  165 us
    dot_general x4, matrix products, attend(): jnp.einsum('tngd,knd->tngk', queries, kr_block, preferred_element_type=jn...  150 us
    dot_general x4, matrix products, attend(): jnp.einsum('tngk,knd->tngd', p_pref.astype(jnp.bfloat16), vp_block, prefe...  87 us
    unnamed x30, local copies, waits for them, and re-layouts  64.5 us
    dot_general x1, matrix products, project_new(): jnp.dot(hidden, w_qkv, preferred_element_type=jnp.float32)  61.4 us
    dot_general x4, matrix products, attend(): jnp.einsum('tngd,knd->tngk', queries, kp_block, preferred_element_type=jn...  58.6 us
  transfers between devices with their start and end apart: 5, of which 1 were waited for; matrix products, arithmetic and copies ran while one was open for 11% of the time, Pallas kernels for 0%

commit v1 on v0

v1 whole, which is shorter than its diff:
```python
import functools

import jax
import jax.numpy as jnp
import numpy as np
from jax import lax
from jax.experimental import pallas as pl
from jax.experimental.pallas import tpu as pltpu
from jax.sharding import PartitionSpec as P


EPS = 1.5625e-07
MASK_VALUE = -1e30
F32 = jnp.float32
BF16 = jnp.bfloat16
LOG2E = 1.4426950408889634
HD = 128
VLIM = 60 * 1024 * 1024


def cost(flops, nbytes):
    return pl.CostEstimate(flops=int(flops), bytes_accessed=int(nbytes), transcendentals=0)


def dot(a, b):
    return jnp.dot(a, b, preferred_element_type=F32)


def norm_kernel(x_ref, g_ref, h_ref):
    x = x_ref[...].astype(F32)
    inv = lax.rsqrt(jnp.mean(x * x, axis=-1, keepdims=True) + EPS)
    h_ref[...] = (x * inv * g_ref[...].astype(F32)).astype(BF16)


def norm(x, g):
    rows, d = x.shape
    rb = 128
    return pl.pallas_call(
        norm_kernel,
        grid=(rows // rb,),
        in_specs=[pl.BlockSpec((rb, d), lambda i: (i, 0)), pl.BlockSpec((1, d), lambda i: (0, 0))],
        out_specs=pl.BlockSpec((rb, d), lambda i: (i, 0)),
        out_shape=jax.ShapeDtypeStruct((rows, d), BF16),
        cost_estimate=cost(rows * d * 80, rows * d * 4),
        name="norm",
    )(x, g.reshape(1, d))


def rotate(v, cos_e, sin_e):
    lane = lax.broadcasted_iota(jnp.int32, v.shape, 1)
    swapped = jnp.where(lane % 2 == 0, pltpu.roll(v, HD - 1, 1), pltpu.roll(v, 1, 1))
    return jnp.where(lane < HD // 2, v * cos_e + swapped * sin_e, v)


MB = 512


def kv_kernel(h_ref, w_ref, b_ref, c_ref, s_ref, k_ref, v_ref, vt_ref):
    bias = b_ref[0].astype(F32)

    @pl.loop(0, h_ref.shape[0] // MB)
    def _(m):
        r = pl.ds(pl.multiple_of(m * MB, MB), MB)
        a = dot(h_ref[r, :], w_ref[...]) + bias
        k_ref[r, :] = rotate(a[:, :HD], c_ref[r, :], s_ref[r, :]).astype(BF16)
        v = a[:, HD:].astype(BF16)
        v_ref[r, :] = v
        vt_ref[:, r] = v.T


def q_kernel(h_ref, w_ref, b_ref, c_ref, s_ref, q_ref):
    bias = b_ref[0].astype(F32)

    @pl.loop(0, h_ref.shape[0] // MB)
    def _(m):
        r = pl.ds(pl.multiple_of(m * MB, MB), MB)
        a = dot(h_ref[r, :], w_ref[...]) + bias
        q_ref[r, :HD] = rotate(a[:, :HD], c_ref[r, :], s_ref[r, :]).astype(BF16)
        q_ref[r, HD:] = rotate(a[:, HD:], c_ref[r, :], s_ref[r, :]).astype(BF16)


def proj_specs(rows, d, col):
    whole = lambda i: (0, 0)
    return [
        pl.BlockSpec((rows, d), whole),
        pl.BlockSpec((d, 2 * HD), lambda i: (0, col(i))),
        pl.BlockSpec((1, 1, 2 * HD), lambda i: (col(i), 0, 0)),
        pl.BlockSpec((rows, HD), whole),
        pl.BlockSpec((rows, HD), whole),
    ]


def project_kv(h, w, b, ce, se, groups):
    rows, d = h.shape
    per = w.shape[1] // (2 * HD * groups)
    col = lambda i: i * per + per - 1
    return pl.pallas_call(
        kv_kernel,
        grid=(groups,),
        in_specs=proj_specs(rows, d, col),
        out_specs=[
            pl.BlockSpec((rows, HD), lambda i: (0, i)),
            pl.BlockSpec((rows, HD), lambda i: (0, i)),
            pl.BlockSpec((HD, rows), lambda i: (i, 0)),
        ],
        out_shape=[
            jax.ShapeDtypeStruct((rows, groups * HD), BF16),
            jax.ShapeDtypeStruct((rows, groups * HD), BF16),
            jax.ShapeDtypeStruct((groups * HD, rows), BF16),
        ],
        compiler_params=pltpu.CompilerParams(vmem_limit_bytes=VLIM),
        cost_estimate=cost(2 * rows * d * groups * 2 * HD, d * groups * 4 * HD + rows * d * 2),
        name="project_kv",
    )(h, w, b, ce, se)


def project_q(h, w, b, ce, se, groups):
    rows, d = h.shape
    per = w.shape[1] // (2 * HD * groups)
    nq = per - 1
    col = lambda i: (i // nq) * per + i % nq
    return pl.pallas_call(
        q_kernel,
        grid=(groups * nq,),
        in_specs=proj_specs(rows, d, col),
        out_specs=pl.BlockSpec((rows, 2 * HD), lambda i: (0, i)),
        out_shape=jax.ShapeDtypeStruct((rows, groups * nq * 2 * HD), BF16),
        compiler_params=pltpu.CompilerParams(vmem_limit_bytes=VLIM),
        cost_estimate=cost(2 * rows * d * groups * nq * 2 * HD, d * groups * nq * 4 * HD + rows * d * 2),
        name="project_q",
    )(h, w, b, ce, se)


QB = 256
KB = 512


def attn_kernel(chunk, group, tok, me_ref, q_ref, kc, vc, ko, vo, ks, vs, kx, vx, kz, vz,
                o_ref, kbuf, vbuf, qt, acc, mrun, lrun, sem):
    g = pl.program_id(0)
    groups = kbuf.shape[0]
    me = me_ref[0]
    pieces = [(None, kc, vc), (0, ko, vo), (1, ks, vs), (2, kx, vx), (3, kz, vz)]

    def each_copy(gg, act):
        for rel, kp, vp in pieces:
            n = kp.shape[0]
            src = None if rel is None else lax.bitwise_xor(me, rel)
            at = 0 if rel is None else pl.multiple_of(kc.shape[0] + src * tok, tok)

            def go(kp=kp, vp=vp, n=n, at=at):
                act(pltpu.make_async_copy(kp.at[:, pl.ds(gg * HD, HD)], kbuf.at[gg, pl.ds(at, n), :], sem.at[gg]))
                act(pltpu.make_async_copy(vp.at[pl.ds(gg * HD, HD), :], vbuf.at[gg, :, pl.ds(at, n)], sem.at[gg]))

            if rel in (None, 0):
                go()
            else:
                pl.when(src < me)(go)

    @pl.when(g == 0)
    def _():
        for gg in range(groups):
            each_copy(gg, lambda c: c.start())

    for h in range(group):
        qt[h] = q_ref[:, h * HD:(h + 1) * HD].T
    acc[...] = jnp.zeros_like(acc)
    lrun[...] = jnp.zeros_like(lrun)
    mrun[...] = jnp.full_like(mrun, MASK_VALUE)

    for gg in range(groups):
        @pl.when(g == gg)
        def _(gg=gg):
            each_copy(gg, lambda c: c.wait())

    conv = LOG2E * HD ** -0.5

    def step(kb, mask):
        k = kbuf[g, pl.ds(pl.multiple_of(kb * KB, KB), KB), :]
        vt = vbuf[g, :, pl.ds(pl.multiple_of(kb * KB, KB), KB)]
        for h in range(group):
            s = dot(k, qt[h])
            if mask is not None:
                s = jnp.where(mask, s, MASK_VALUE)
            m_old = mrun[h]
            m_new = jnp.maximum(m_old, jnp.max(s, axis=0, keepdims=True))
            p = jnp.exp2(s * conv - m_new * conv)
            alpha = jnp.exp2((m_old - m_new) * conv)
            mrun[h] = m_new
            lrun[h] = lrun[h] * alpha + p.reshape(KB // 8, 8, QB).sum(axis=0)
            acc[h] = acc[h] * alpha + dot(vt, p.astype(BF16))

    first = kc.shape[0] + me * tok + chunk * QB
    nfull = first // KB

    @pl.loop(0, nfull)
    def _(kb):
        step(kb, None)

    off = (kc.shape[0] + chunk * QB) % KB
    key = lax.broadcasted_iota(jnp.int32, (KB, QB), 0)
    row = lax.broadcasted_iota(jnp.int32, (KB, QB), 1)
    step(nfull, key <= row + off)

    for h in range(group):
        total = jnp.sum(lrun[h], axis=0, keepdims=True)
        o_ref[:, h * HD:(h + 1) * HD] = (acc[h] / total).T.astype(BF16)


def attend(chunk, me, q, pieces, group):
    tok, width = q.shape
    groups = width // (group * HD)
    ncache = pieces[0].shape[0]
    total = ncache + 4 * tok
    anyspec = pl.BlockSpec(memory_space=pl.ANY)
    return pl.pallas_call(
        functools.partial(attn_kernel, chunk, group, tok),
        grid_spec=pltpu.PrefetchScalarGridSpec(
            num_scalar_prefetch=1,
            grid=(groups,),
            in_specs=[pl.BlockSpec((QB, group * HD), lambda g, me: (chunk, g))] + [anyspec] * 10,
            out_specs=pl.BlockSpec((QB, group * HD), lambda g, me: (0, g)),
            scratch_shapes=[
                pltpu.VMEM((groups, total, HD), BF16),
                pltpu.VMEM((groups, HD, total), BF16),
                pltpu.VMEM((group, HD, QB), BF16),
                pltpu.VMEM((group, HD, QB), F32),
                pltpu.VMEM((group, 1, QB), F32),
                pltpu.VMEM((group, 8, QB), F32),
                pltpu.SemaphoreType.DMA((groups,)),
            ],
        ),
        out_shape=jax.ShapeDtypeStruct((QB, width), BF16),
        compiler_params=pltpu.CompilerParams(vmem_limit_bytes=VLIM),
        cost_estimate=cost(40e9, 12e6),
    )(me, q, *pieces)


def own_kernel(nchunk, x_ref, w_ref, *refs):
    chunks, (y_ref, obuf, sem) = refs[:nchunk], refs[nchunk:]
    rows = chunks[0].shape[0]

    @pl.when(pl.program_id(0) == 0)
    def _():
        copies = [pltpu.make_async_copy(c, obuf.at[pl.ds(i * rows, rows), :], sem.at[i]) for i, c in enumerate(chunks)]
        for c in copies:
            c.start()
        for c in copies:
            c.wait()

    @pl.loop(0, obuf.shape[0] // MB)
    def _(m):
        r = pl.ds(pl.multiple_of(m * MB, MB), MB)
        y_ref[r, :] = x_ref[r, :].astype(F32) + dot(obuf[r, :], w_ref[...])


def own_part(x, w, chunks):
    rows, d = x.shape
    inner = w.shape[0]
    nb = 512
    return pl.pallas_call(
        functools.partial(own_kernel, len(chunks)),
        grid=(d // nb,),
        in_specs=[
            pl.BlockSpec((rows, nb), lambda i: (0, i)),
            pl.BlockSpec((inner, nb), lambda i: (0, i)),
        ] + [pl.BlockSpec(memory_space=pl.ANY)] * len(chunks),
        out_specs=pl.BlockSpec((rows, nb), lambda i: (0, i)),
        out_shape=jax.ShapeDtypeStruct((rows, d), F32),
        scratch_shapes=[pltpu.VMEM((rows, inner), BF16), pltpu.SemaphoreType.DMA((len(chunks),))],
        compiler_params=pltpu.CompilerParams(vmem_limit_bytes=VLIM),
        cost_estimate=cost(2 * rows * inner * d, rows * d * 6 + inner * d * 2),
        name="own_part",
    )(x, w, *chunks)


def other_kernel(nper, me_ref, o_ref, a_ref, *refs):
    me = me_ref[0]
    ws, y_ref = refs[:4 * nper], refs[-1]
    wr = ws[0].shape[0]
    total = a_ref[...]
    for i in range(4 * nper):
        quarter = lax.bitwise_xor(me, i // nper)
        at = pl.multiple_of(quarter * (nper * wr) + (i % nper) * wr, wr)
        total = total + dot(o_ref[:, pl.ds(at, wr)], ws[i][...])
    y_ref[...] = total.astype(BF16)


def other_part(chunk, me, o, partial, ws, y):
    rows = o.shape[0]
    d = partial.shape[1]
    nb = 512
    wr = ws[0].shape[0]
    extra = [] if y is None else [y]
    return pl.pallas_call(
        functools.partial(other_kernel, len(ws) // 4),
        grid_spec=pltpu.PrefetchScalarGridSpec(
            num_scalar_prefetch=1,
            grid=(d // nb,),
            in_specs=[
                pl.BlockSpec(o.shape, lambda i, me: (0, 0)),
                pl.BlockSpec((rows, nb), lambda i, me: (chunk, i)),
            ] + [pl.BlockSpec((wr, nb), lambda i, me: (0, i))] * len(ws)
            + [pl.BlockSpec(memory_space=pl.ANY)] * len(extra),
            out_specs=pl.BlockSpec((rows, nb), lambda i, me: (chunk, i)),
        ),
        out_shape=jax.ShapeDtypeStruct(partial.shape, BF16),
        input_output_aliases={} if y is None else {3 + len(ws): 0},
        compiler_params=pltpu.CompilerParams(vmem_limit_bytes=VLIM),
        cost_estimate=cost(2 * rows * wr * len(ws) * d, rows * d * 6 + wr * len(ws) * d * 2),
    )(me, o, partial, *ws, *extra)


def cp_send(v, rel):
    return lax.ppermute(v, 'cp', [(i, i ^ rel) for i in range(4)])


def tp_send(v):
    return lax.ppermute(v, 'tp', [(0, 1), (1, 0)])


def spread_matrices(half, hd):
    out = np.zeros((2 * half, 2 * hd), np.float32)
    for lane in range(2 * half):
        out[lane // 2, lane] = 1.0
        out[half + lane // 2, hd + lane] = 1.0 if lane % 2 else -1.0
    return out


def block(x, k_cache, v_cache, rope_table, norm_gain, w_qkv, b_qkv, w_out):
    tok, d = x.shape
    ncache, groups, hd = k_cache.shape
    group = w_qkv.shape[1] // (groups * hd) - 2
    cp = lax.axis_index('cp')
    me = cp.astype(jnp.int32).reshape(1)
    bar = lax.optimization_barrier

    nper = 3
    wr = w_out.shape[0] // (4 * nper)
    w_parts = [lax.dynamic_slice(w_out, (cp * (nper * wr) + i * wr, 0), (wr, d)) for i in range(nper)]
    wy = [tp_send(p) for p in w_parts]

    cache = jnp.concatenate([k_cache.reshape(ncache, groups * hd), v_cache.reshape(ncache, groups * hd)], axis=1)
    caches = jnp.concatenate([cache] + [cp_send(cache, r) for r in (1, 2, 3)], axis=0)
    kc = caches[:, :groups * hd]
    vc = caches[:, groups * hd:].T

    half = rope_table.shape[1] // 2
    spread = jnp.dot(rope_table, spread_matrices(half, hd), precision=lax.Precision.HIGHEST)
    ce, se = spread[:, :hd], spread[:, hd:]
    bias = b_qkv.reshape(-1, 1, 2 * hd)

    h = norm(x, norm_gain)
    k, v, vt = project_kv(h, w_qkv, bias, ce, se, groups)
    ks, vs = cp_send(k, 1), cp_send(vt, 1)
    kx, vx = cp_send(k, 2), cp_send(vt, 2)
    q = project_q(h, w_qkv, bias, ce, se, groups)
    (q, kx, vx, wy[0]) = bar((q, kx, vx, wy[0]))
    kz, vz = cp_send(kx, 1), cp_send(vx, 1)
    pieces = [kc, vc, k, vt, ks, vs, kx, vx, kz, vz]

    wx, wd, wz = [None] * nper, [None] * nper, [None] * nper

    def forward(i):
        wx[i], wd[i] = cp_send(wy[i], 2), cp_send(wy[i], 1)

    def relay(i):
        wz[i] = cp_send(wx[i], 1)

    forward(0)
    outs, others = [], []
    for chunk in range(tok // QB):
        o = attend(chunk, me, q, pieces, group)
        if chunk == 1:
            (o, q, wy[1], wx[0]) = bar((o, q, wy[1], wx[0]))
            forward(1)
            relay(0)
        elif chunk == 3:
            (o, q, wy[2], wx[1]) = bar((o, q, wy[2], wx[1]))
            forward(2)
            relay(1)
        else:
            (o, q) = bar((o, q))
        outs.append(o)
        others.append(tp_send(o))

    partial = own_part(x, w_out, outs)
    (partial, wx[2]) = bar((partial, wx[2]))
    relay(2)
    ws = wy + wd + wx + wz
    y = None
    for chunk in range(tok // QB):
        y = other_part(chunk, me, others[chunk], partial, ws, y)
    return y, k.reshape(tok, groups, hd), v.reshape(tok, groups, hd)


def solution(mesh):
    row_spec = P(('dp', 'cp'), None)
    cache_spec = P(('dp', 'cp'), 'tp', None)
    return jax.shard_map(block, mesh=mesh, in_specs=(row_spec, cache_spec, cache_spec, row_spec, P(None), P(None, 'tp'), P('tp'), P('tp', None)), out_specs=(row_spec, cache_spec, cache_spec), check_vma=False)
```

time: 1470 us -> 758 us (0.52)
  matrix products: 570 us -> 1.87 us
  waiting for transfers between devices: 547 us -> 120 us
  Pallas kernels: 0 us -> 390 us
  other arithmetic: 224 us -> 4.18 us
  starting transfers between devices: 0.46 us -> 219 us
  local copies, waits for them, and re-layouts: 93.3 us -> 20.7 us
  loops' own time: 14.9 us -> 0 us
    dot_general x18 -> x1, matrix products: 570 us -> 1.87 us  [block(): jnp.dot(rope_table, spread_matrices(half, hd), precision=lax.Precision.HI...]
    psum x1 -> x0, waiting for transfers between devices: 547 us -> none  [local_step(): y = (x_f32 + lax.psum(proj_part, 'tp')).astype(jnp.bfloat16)]
    pallas_call x0 -> x12, Pallas kernels: none -> 390 us  [the longest x4 162 us: attend(): pl.pallas_call(functools.partial(attn_kernel, chunk, group, tok), grid_sp...]
    ppermute x0 -> x25, starting transfers between devices: none -> 219 us  [the longest x18 211 us: cp_send(): return lax.ppermute(v, 'cp', [(i, i ^ rel) for i in range(4)])]
    reduce_sum x9 -> x0, other arithmetic: 174 us -> none  [the longest x8 167 us: attend(): run_sum = run_sum * rescale + p_pref.sum(axis=-1) + p_recent.sum(axis=-1)]
    ppermute x0 -> x25, waiting for transfers between devices: none -> 120 us  [the longest x7 82 us: tp_send(): return lax.ppermute(v, 'tp', [(0, 1), (1, 0)])]
    unnamed x30 -> x16, local copies, waits for them, and re-layouts: 64.5 us -> 2.72 us
    convert_element_type x6 -> x0, other arithmetic: 29.1 us -> none  [the longest x1 17.1 us: local_step(): y = (x_f32 + lax.psum(proj_part, 'tp')).astype(jnp.bfloat16)]
  transfers between devices with their start and end apart: 5 -> 25, of which waited for: 1 -> 8; matrix products, arithmetic and copies ran while one was open for 11% -> 2% of each run, Pallas kernels for 0% -> 44%
where the time goes in v1:
time: 758 us
  Pallas kernels  390 us (51%)
  starting transfers between devices  219 us (29%)
  waiting for transfers between devices  120 us (16%)
  local copies, waits for them, and re-layouts  20.7 us (3%)
    ppermute x18, starting transfers between devices, cp_send(): return lax.ppermute(v, 'cp', [(i, i ^ rel) for i in range(4)])  211 us
    pallas_call x4, Pallas kernels, attend(): pl.pallas_call(functools.partial(attn_kernel, chunk, group, tok), grid_sp...  162 us
    pallas_call x4, Pallas kernels, other_part(): pl.pallas_call(functools.partial(other_kernel, len(ws) // 4), grid_spec=p...  87.3 us
    ppermute x7, waiting for transfers between devices, tp_send(): return lax.ppermute(v, 'tp', [(0, 1), (1, 0)])  82 us
    pallas_call x1, Pallas kernels, project_q(): pl.pallas_call(q_kernel, grid=(groups * nq,), in_specs=proj_specs(rows, d...  55.1 us
    pallas_call x1, Pallas kernels, own_part(): pl.pallas_call(functools.partial(own_kernel, len(chunks)), grid=(d // nb,...  50.1 us
    ppermute x18, waiting for transfers between devices, cp_send(): return lax.ppermute(v, 'cp', [(i, i ^ rel) for i in range(4)])  38.4 us
    pallas_call x1, Pallas kernels, project_kv(): pl.pallas_call(kv_kernel, grid=(groups,), in_specs=proj_specs(rows, d, co...  22.2 us
  transfers between devices with their start and end apart: 25, of which 8 were waited for; matrix products, arithmetic and copies ran while one was open for 2% of the time, Pallas kernels for 44%

profile of v1, /device:TPU:0, one launch (start us, length us, event | category | flops | bytes accessed | tf_op | source)
XLA Modules:
  0.0 757.5 jit_solution(7532086803575997016)
XLA Ops:
  3.3 1.9 convolution_bitcast_fusion
  6.2 13.9 %norm.1.h_ref = bf16[1024,6144]{1,0:T(8,128)(2,1)} custom-call(bf16[1024,6144]{1,0:T(8,128)(2,1)} %x_ref.3, bf16[1,6144]{1,0:T(2,128)(2,1)} %reshape.28.g_ref), custom_call_target="tpu_custom_call" | custom-call | flops 503316480 | bytes 25165824 | tf_op jit(solution)/shard_map/norm/pallas_call | solution.py:38
  20.2 22.2 %project_kv.1 = (bf16[1024,512]{1,0:T(8,128)(2,1)}, bf16[1024,512]{1,0:T(8,128)(2,1)}, bf16[512,1024]{1,0:T(8,128)(2,1)}) custom-call(bf16[1024,6144]{1,0:T(8,128)(2,1)} %norm.1.h_ref, bf16[6144,4096]{1,0:T(8,128)(2,1)} %w_ref.4, bf16[16,1,256]{2,1,0:T(2,128)(2,1)} %reshape.34.b_ref, f32[1024,128]{1,0:T(8,128)} %get-tuple-element.49.c_ref, ...), custom_call_target="tpu_custom_call" | custom-call | flops 12884901888 | bytes 25165824 | tf_op jit(solution)/shard_map/project_kv/pallas_call | solution.py:97
  42.4 3.3 collective-permute-start.1
  48.7 7.6 constant_dynamic-slice_fusion
  56.3 1.5 collective-permute-start.2
  57.8 12.2 %collective-permute-done.1.vx = bf16[512,1024]{1,0:T(8,128)(2,1)} collective-permute-done((bf16[512,1024]{1,0:T(8,128)(2,1)}, bf16[512,1024]{1,0:T(8,128)(2,1)}, u32[]{:S(2)}, u32[]{:S(2)}) %collective-permute-start.1) | collective-permute-done | bytes 1048608 | tf_op jit(solution)/shard_map/ppermute | solution.py:315
  70.0 2.0 collective-permute-start
  72.0 55.1 %project_q.1.q_ref = bf16[1024,3072]{1,0:T(8,128)(2,1)} custom-call(bf16[1024,6144]{1,0:T(8,128)(2,1)} %norm.1.h_ref, bf16[6144,4096]{1,0:T(8,128)(2,1)} %w_ref.4, bf16[16,1,256]{2,1,0:T(2,128)(2,1)} %reshape.34.b_ref, f32[1024,128]{1,0:T(8,128)} %get-tuple-element.49.c_ref, f32[1024,128]{1,0:T(8,128)} %get-tuple-element.48.s_ref), custom_call_target="tpu_custom_call" | custom-call | flops 38654705664 | bytes 50331648 | tf_op jit(solution)/shard_map/project_q/pallas_call | solution.py:122
  128.2 1.5 collective-permute-start.12
  129.7 3.4 pad_maximum_fusion
  136.2 34.1 %shard_map.112.refs_0_ = bf16[256,3072]{1,0:T(8,128)(2,1)} custom-call(s32[1]{0:T(128)} %bitcast.me_ref, bf16[1024,3072]{1,0:T(8,128)(2,1)} %project_q.1.q_ref, bf16[1024,512]{1,0:T(8,128)(2,1)} %copy.27.kc, bf16[512,1024]{1,0:T(8,128)(2,1)} %get-tuple-element.46.vc, bf16[1024,512]{1,0:T(8,128)(2,1)} %get-tuple-element.23.ko, ...), custom_call_target="tpu_custom_call" | custom-call | flops 40000000000 | bytes 12000000 | tf_op jit(solution)/shard_map/pallas_call | solution.py:216
  170.3 2.0 collective-permute-start.24
  172.3 35.9 %shard_map.113.refs_1_ = bf16[256,3072]{1,0:T(8,128)(2,1)} custom-call(s32[1]{0:T(128)} %bitcast.me_ref, bf16[1024,3072]{1,0:T(8,128)(2,1)} %project_q.1.q_ref, bf16[1024,512]{1,0:T(8,128)(2,1)} %copy.27.kc, bf16[512,1024]{1,0:T(8,128)(2,1)} %get-tuple-element.46.vc, bf16[1024,512]{1,0:T(8,128)(2,1)} %get-tuple-element.23.ko, ...), custom_call_target="tpu_custom_call" | custom-call | flops 40000000000 | bytes 12000000 | tf_op jit(solution)/shard_map/pallas_call | solution.py:216
  208.2 58.6 %collective-permute-done.10.refs_1_ = bf16[256,6144]{1,0:T(8,128)(2,1)S(1)} collective-permute-done((bf16[256,6144]{1,0:T(8,128)(2,1)}, bf16[256,6144]{1,0:T(8,128)(2,1)S(1)}, u32[]{:S(2)}, u32[]{:S(2)}) %collective-permute-start.10) | collective-permute-done | bytes 3145760 | tf_op jit(solution)/shard_map/ppermute | solution.py:319
  266.8 72.4 %collective-permute-start.13 = (bf16[256,6144]{1,0:T(8,128)(2,1)S(1)}, bf16[256,6144]{1,0:T(8,128)(2,1)}, u32[]{:S(2)}, u32[]{:S(2)}) collective-permute-start(bf16[256,6144]{1,0:T(8,128)(2,1)S(1)} %collective-permute-done.10.refs_1_), channel_id=1, source_target_pairs={{0,2},{1,3},{2,0},{3,1},{4,6},{5,7},{6,4},{7,5}} | collective-permute-start | bytes 9437192 | tf_op jit(solution)/shard_map/ppermute | solution.py:315
  339.2 44.9 %shard_map.114.refs_2_ = bf16[256,3072]{1,0:T(8,128)(2,1)} custom-call(s32[1]{0:T(128)} %bitcast.me_ref, bf16[1024,3072]{1,0:T(8,128)(2,1)} %project_q.1.q_ref, bf16[1024,512]{1,0:T(8,128)(2,1)} %copy.27.kc, bf16[512,1024]{1,0:T(8,128)(2,1)} %get-tuple-element.46.vc, bf16[1024,512]{1,0:T(8,128)(2,1)} %get-tuple-element.23.ko, ...), custom_call_target="tpu_custom_call" | custom-call | flops 40000000000 | bytes 12000000 | tf_op jit(solution)/shard_map/pallas_call | solution.py:216
  384.1 46.6 %shard_map.115.refs_3_ = bf16[256,3072]{1,0:T(8,128)(2,1)} custom-call(s32[1]{0:T(128)} %bitcast.me_ref, bf16[1024,3072]{1,0:T(8,128)(2,1)} %project_q.1.q_ref, bf16[1024,512]{1,0:T(8,128)(2,1)} %copy.27.kc, bf16[512,1024]{1,0:T(8,128)(2,1)} %get-tuple-element.46.vc, bf16[1024,512]{1,0:T(8,128)(2,1)} %get-tuple-element.23.ko, ...), custom_call_target="tpu_custom_call" | custom-call | flops 40000000000 | bytes 12000000 | tf_op jit(solution)/shard_map/pallas_call | solution.py:216
  430.8 43.0 %collective-permute-start.19 = (bf16[256,6144]{1,0:T(8,128)(2,1)}, bf16[256,6144]{1,0:T(8,128)(2,1)}, u32[]{:S(2)}, u32[]{:S(2)}) collective-permute-start(bf16[256,6144]{1,0:T(8,128)(2,1)} %collective-permute-done.11.refs_6_), channel_id=1, source_target_pairs={{0,1},{1,0},{2,3},{3,2},{4,5},{5,4},{6,7},{7,6}} | collective-permute-start | bytes 9437192 | tf_op jit(solution)/shard_map/ppermute | solution.py:315
  473.7 87.0 %collective-permute-start.15 = (bf16[256,6144]{1,0:T(8,128)(2,1)}, bf16[256,6144]{1,0:T(8,128)(2,1)}, u32[]{:S(2)}, u32[]{:S(2)}) collective-permute-start(bf16[256,6144]{1,0:T(8,128)(2,1)} %collective-permute-done.12.refs_2_), channel_id=1, source_target_pairs={{0,2},{1,3},{2,0},{3,1},{4,6},{5,7},{6,4},{7,5}} | collective-permute-start | bytes 9437192 | tf_op jit(solution)/shard_map/ppermute | solution.py:315
  560.7 50.1 %own_part.1.a_ref = f32[1024,6144]{1,0:T(8,128)} custom-call(bf16[1024,6144]{1,0:T(8,128)(2,1)} %x_ref.3, bf16[3072,6144]{1,0:T(8,128)(2,1)} %w_ref.5, bf16[256,3072]{1,0:T(8,128)(2,1)} %shard_map.112.refs_0_, bf16[256,3072]{1,0:T(8,128)(2,1)} %shard_map.113.refs_1_, bf16[256,3072]{1,0:T(8,128)(2,1)} %shard_map.114.refs_2_, bf16[256,3072]{1,0:T(8,128)(2,1)} %shard_map.115.refs_3_), custom_call_target="tpu_custom_call" | custom-call | flops 38654705664 | bytes 75497472 | tf_op jit(solution)/shard_map/own_part/pallas_call | solution.py:261
  610.8 18.5 %collective-permute-done.15.refs_8_ = bf16[256,6144]{1,0:T(8,128)(2,1)} collective-permute-done((bf16[256,6144]{1,0:T(8,128)(2,1)}, bf16[256,6144]{1,0:T(8,128)(2,1)}, u32[]{:S(2)}, u32[]{:S(2)}) %collective-permute-start.15) | collective-permute-done | bytes 3145760 | tf_op jit(solution)/shard_map/ppermute | solution.py:315
  630.4 2.1 reshape.32
  632.5 2.1 reshape.33
  636.2 3.7 collective-permute-done.20.refs_10_
  640.4 4.0 collective-permute-done.21.refs_11_
  644.3 21.8 %shard_map.116.refs_12_ = bf16[1024,6144]{1,0:T(8,128)(2,1)} custom-call(s32[1]{0:T(128)} %bitcast.me_ref, bf16[256,3072]{1,0:T(8,128)(2,1)} %collective-permute-done.24.o_ref, f32[1024,6144]{1,0:T(8,128)} %own_part.1.a_ref, bf16[256,6144]{1,0:T(8,128)(2,1)} %collective-permute-done.2.refs_0_, bf16[256,6144]{1,0:T(8,128)(2,1)} %copy-done.2, ...), custom_call_target="tpu_custom_call" | custom-call | flops 9663676416 | bytes 47185920 | tf_op jit(solution)/shard_map/pallas_call | solution.py:295
  667.5 21.8 %shard_map.117.refs_12_ = bf16[1024,6144]{1,0:T(8,128)(2,1)} custom-call(s32[1]{0:T(128)} %bitcast.me_ref, bf16[256,3072]{1,0:T(8,128)(2,1)} %collective-permute-done.23.o_ref, f32[1024,6144]{1,0:T(8,128)} %own_part.1.a_ref, bf16[256,6144]{1,0:T(8,128)(2,1)} %collective-permute-done.2.refs_0_, ...), custom_call_target="tpu_custom_call", output_to_operand_aliasing={{}: (15, {})} | custom-call | flops 9663676416 | bytes 47185920 | tf_op jit(solution)/shard_map/pallas_call | solution.py:295
  689.3 11.8 %collective-permute-done.22.o_ref = bf16[256,3072]{1,0:T(8,128)(2,1)S(1)} collective-permute-done((bf16[256,3072]{1,0:T(8,128)(2,1)}, bf16[256,3072]{1,0:T(8,128)(2,1)S(1)}, u32[]{:S(2)}, u32[]{:S(2)}) %collective-permute-start.22) | collective-permute-done | bytes 1572896 | tf_op jit(solution)/shard_map/ppermute | solution.py:319
  702.3 21.8 %shard_map.118.refs_12_ = bf16[1024,6144]{1,0:T(8,128)(2,1)} custom-call(s32[1]{0:T(128)} %bitcast.me_ref, bf16[256,3072]{1,0:T(8,128)(2,1)} %copy-done.4, f32[1024,6144]{1,0:T(8,128)} %own_part.1.a_ref, bf16[256,6144]{1,0:T(8,128)(2,1)} %collective-permute-done.2.refs_0_, bf16[256,6144]{1,0:T(8,128)(2,1)} %copy-done.2, ...), custom_call_target="tpu_custom_call", output_to_operand_aliasing={{}: (15, {})} | custom-call | flops 9663676416 | bytes 47185920 | tf_op jit(solution)/shard_map/pallas_call | solution.py:295
  724.1 10.2 %collective-permute-done.14.o_ref = bf16[256,3072]{1,0:T(8,128)(2,1)S(1)} collective-permute-done((bf16[256,3072]{1,0:T(8,128)(2,1)}, bf16[256,3072]{1,0:T(8,128)(2,1)S(1)}, u32[]{:S(2)}, u32[]{:S(2)}) %collective-permute-start.14) | collective-permute-done | bytes 1572896 | tf_op jit(solution)/shard_map/ppermute | solution.py:319
  735.5 21.8 %shard_map.119 = bf16[1024,6144]{1,0:T(8,128)(2,1)} custom-call(s32[1]{0:T(128)} %bitcast.me_ref, bf16[256,3072]{1,0:T(8,128)(2,1)} %copy-done.3, f32[1024,6144]{1,0:T(8,128)} %own_part.1.a_ref, bf16[256,6144]{1,0:T(8,128)(2,1)} %collective-permute-done.2.refs_0_, bf16[256,6144]{1,0:T(8,128)(2,1)} %copy-done.2, ...), custom_call_target="tpu_custom_call", output_to_operand_aliasing={{}: (15, {})} | custom-call | flops 9663676416 | bytes 47185920 | tf_op jit(solution)/shard_map/pallas_call | solution.py:295
  (57 shorter events, 17.6 us)
Async XLA Ops:
  0.6 2.7 copy-start
  20.1 25.5 %copy-start.5 = (bf16[256,4,128]{2,1,0:T(4,128)(2,1)S(1)}, bf16[256,4,128]{2,1,0:T(4,128)(2,1)}, u32[]{:S(2)}) copy-start(bf16[256,4,128]{2,1,0:T(4,128)(2,1)} %param.10) | copy-start | bytes 786436
  20.2 25.7 %copy-start.6 = (bf16[256,4,128]{2,1,0:T(4,128)(2,1)S(1)}, bf16[256,4,128]{2,1,0:T(4,128)(2,1)}, u32[]{:S(2)}) copy-start(bf16[256,4,128]{2,1,0:T(4,128)(2,1)} %param.11) | copy-start | bytes 786436
  42.4 27.6 %collective-permute-start.1 = (bf16[512,1024]{1,0:T(8,128)(2,1)}, bf16[512,1024]{1,0:T(8,128)(2,1)}, u32[]{:S(2)}, u32[]{:S(2)}) collective-permute-start(bf16[512,1024]{1,0:T(8,128)(2,1)} %get-tuple-element.24.vo), channel_id=1, source_target_pairs={{0,2},{1,3},{2,0},{3,1},{4,6},{5,7},{6,4},{7,5}} | collective-permute-start | bytes 3145736 | tf_op jit(solution)/shard_map/ppermute | solution.py:315
  46.9 80.8 %collective-permute-start.5 = (bf16[256,1024]{0,1:T(8,128)(2,1)}, bf16[256,1024]{0,1:T(8,128)(2,1)}, u32[]{:S(2)}, u32[]{:S(2)}) collective-permute-start(bf16[256,1024]{0,1:T(8,128)(2,1)} %pad_maximum_fusion.1), channel_id=1, source_target_pairs={{0,3},{1,2},{2,1},{3,0},{4,7},{5,6},{6,5},{7,4}} | collective-permute-start | bytes 1572872 | tf_op jit(solution)/shard_map/ppermute | solution.py:315
  46.9 80.9 %collective-permute-start.4 = (bf16[256,1024]{0,1:T(8,128)(2,1)}, bf16[256,1024]{0,1:T(8,128)(2,1)}, u32[]{:S(2)}, u32[]{:S(2)}) collective-permute-start(bf16[256,1024]{0,1:T(8,128)(2,1)} %pad_maximum_fusion.1), channel_id=1, source_target_pairs={{0,2},{1,3},{2,0},{3,1},{4,6},{5,7},{6,4},{7,5}} | collective-permute-start | bytes 1572872 | tf_op jit(solution)/shard_map/ppermute | solution.py:315
  48.1 80.2 %collective-permute-start.3 = (bf16[256,1024]{0,1:T(8,128)(2,1)}, bf16[256,1024]{0,1:T(8,128)(2,1)}, u32[]{:S(2)}, u32[]{:S(2)}) collective-permute-start(bf16[256,1024]{0,1:T(8,128)(2,1)} %pad_maximum_fusion.1), channel_id=1, source_target_pairs={{0,1},{1,0},{2,3},{3,2},{4,5},{5,4},{6,7},{7,6}} | collective-permute-start | bytes 1572872 | tf_op jit(solution)/shard_map/ppermute | solution.py:315
  56.3 70.9 %collective-permute-start.2 = (bf16[256,6144]{1,0:T(8,128)(2,1)S(1)}, bf16[256,6144]{1,0:T(8,128)(2,1)}, u32[]{:S(2)}, u32[]{:S(2)}) collective-permute-start(bf16[256,6144]{1,0:T(8,128)(2,1)S(1)} %get-tuple-element.45), channel_id=1, source_target_pairs={{0,4},{4,0},{1,5},{5,1},{2,6},{6,2},{3,7},{7,3}} | collective-permute-start | bytes 9437192 | tf_op jit(solution)/shard_map/ppermute | solution.py:319
  70.0 57.2 %collective-permute-start = (bf16[1024,512]{1,0:T(8,128)(2,1)}, bf16[1024,512]{1,0:T(8,128)(2,1)}, u32[]{:S(2)}, u32[]{:S(2)}) collective-permute-start(bf16[1024,512]{1,0:T(8,128)(2,1)} %get-tuple-element.23.ko), channel_id=1, source_target_pairs={{0,2},{1,3},{2,0},{3,1},{4,6},{5,7},{6,4},{7,5}} | collective-permute-start | bytes 3145736 | tf_op jit(solution)/shard_map/ppermute | solution.py:315
  127.2 8.4 %collective-permute-start.7 = (bf16[512,1024]{1,0:T(8,128)(2,1)}, bf16[512,1024]{1,0:T(8,128)(2,1)}, u32[]{:S(2)}, u32[]{:S(2)}) collective-permute-start(bf16[512,1024]{1,0:T(8,128)(2,1)} %get-tuple-element.24.vo), channel_id=1, source_target_pairs={{0,1},{1,0},{2,3},{3,2},{4,5},{5,4},{6,7},{7,6}} | collective-permute-start | bytes 3145736 | tf_op jit(solution)/shard_map/ppermute | solution.py:315
  127.2 8.9 %collective-permute-start.6 = (bf16[1024,512]{1,0:T(8,128)(2,1)}, bf16[1024,512]{1,0:T(8,128)(2,1)}, u32[]{:S(2)}, u32[]{:S(2)}) collective-permute-start(bf16[1024,512]{1,0:T(8,128)(2,1)} %get-tuple-element.23.ko), channel_id=1, source_target_pairs={{0,1},{1,0},{2,3},{3,2},{4,5},{5,4},{6,7},{7,6}} | collective-permute-start | bytes 3145736 | tf_op jit(solution)/shard_map/ppermute | solution.py:315
  127.7 8.4 %collective-permute-start.8 = (bf16[1024,512]{1,0:T(8,128)(2,1)}, bf16[1024,512]{1,0:T(8,128)(2,1)}, u32[]{:S(2)}, u32[]{:S(2)}) collective-permute-start(bf16[1024,512]{1,0:T(8,128)(2,1)} %collective-permute-done.kx), channel_id=1, source_target_pairs={{0,1},{1,0},{2,3},{3,2},{4,5},{5,4},{6,7},{7,6}} | collective-permute-start | bytes 3145736 | tf_op jit(solution)/shard_map/ppermute | solution.py:315
  127.7 8.4 %collective-permute-start.9 = (bf16[512,1024]{1,0:T(8,128)(2,1)}, bf16[512,1024]{1,0:T(8,128)(2,1)}, u32[]{:S(2)}, u32[]{:S(2)}) collective-permute-start(bf16[512,1024]{1,0:T(8,128)(2,1)} %collective-permute-done.1.vx), channel_id=1, source_target_pairs={{0,1},{1,0},{2,3},{3,2},{4,5},{5,4},{6,7},{7,6}} | collective-permute-start | bytes 3145736 | tf_op jit(solution)/shard_map/ppermute | solution.py:315
  128.2 302.6 %collective-permute-start.12 = (bf16[256,6144]{1,0:T(8,128)(2,1)}, bf16[256,6144]{1,0:T(8,128)(2,1)}, u32[]{:S(2)}, u32[]{:S(2)}) collective-permute-start(bf16[256,6144]{1,0:T(8,128)(2,1)} %get-tuple-element.43), channel_id=1, source_target_pairs={{0,4},{4,0},{1,5},{5,1},{2,6},{6,2},{3,7},{7,3}} | collective-permute-start | bytes 9437192 | tf_op jit(solution)/shard_map/ppermute | solution.py:319
  135.6 131.2 %collective-permute-start.10 = (bf16[256,6144]{1,0:T(8,128)(2,1)}, bf16[256,6144]{1,0:T(8,128)(2,1)S(1)}, u32[]{:S(2)}, u32[]{:S(2)}) collective-permute-start(bf16[256,6144]{1,0:T(8,128)(2,1)} %get-tuple-element.44), channel_id=1, source_target_pairs={{0,4},{4,0},{1,5},{5,1},{2,6},{6,2},{3,7},{7,3}} | collective-permute-start | bytes 9437192 | tf_op jit(solution)/shard_map/ppermute | solution.py:319
  136.1 493.8 %collective-permute-start.16 = (bf16[256,6144]{1,0:T(8,128)(2,1)}, bf16[256,6144]{1,0:T(8,128)(2,1)}, u32[]{:S(2)}, u32[]{:S(2)}) collective-permute-start(bf16[256,6144]{1,0:T(8,128)(2,1)} %collective-permute-done.2.refs_0_), channel_id=1, source_target_pairs={{0,1},{1,0},{2,3},{3,2},{4,5},{5,4},{6,7},{7,6}} | collective-permute-start | bytes 9437192 | tf_op jit(solution)/shard_map/ppermute | solution.py:315
  136.1 130.7 %collective-permute-start.11 = (bf16[256,6144]{1,0:T(8,128)(2,1)}, bf16[256,6144]{1,0:T(8,128)(2,1)}, u32[]{:S(2)}, u32[]{:S(2)}) collective-permute-start(bf16[256,6144]{1,0:T(8,128)(2,1)} %collective-permute-done.2.refs_0_), channel_id=1, source_target_pairs={{0,2},{1,3},{2,0},{3,1},{4,6},{5,7},{6,4},{7,5}} | collective-permute-start | bytes 9437192 | tf_op jit(solution)/shard_map/ppermute | solution.py:315
  170.3 459.0 %collective-permute-start.24 = (bf16[256,3072]{1,0:T(8,128)(2,1)}, bf16[256,3072]{1,0:T(8,128)(2,1)}, u32[]{:S(2)}, u32[]{:S(2)}) collective-permute-start(bf16[256,3072]{1,0:T(8,128)(2,1)} %shard_map.112.refs_0_), channel_id=1, source_target_pairs={{0,4},{4,0},{1,5},{5,1},{2,6},{6,2},{3,7},{7,3}} | collective-permute-start | bytes 4718600 | tf_op jit(solution)/shard_map/ppermute | solution.py:319
  266.8 117.3 %copy-start.2 = (bf16[256,6144]{1,0:T(8,128)(2,1)}, bf16[256,6144]{1,0:T(8,128)(2,1)S(1)}, u32[]{:S(2)}) copy-start(bf16[256,6144]{1,0:T(8,128)(2,1)S(1)} %collective-permute-done.10.refs_1_) | copy-start | bytes 9437188
  266.8 367.8 %collective-permute-start.17 = (bf16[256,6144]{1,0:T(8,128)(2,1)S(1)}, bf16[256,6144]{1,0:T(8,128)(2,1)}, u32[]{:S(2)}, u32[]{:S(2)}) collective-permute-start(bf16[256,6144]{1,0:T(8,128)(2,1)S(1)} %collective-permute-done.10.refs_1_), channel_id=1, source_target_pairs={{0,1},{1,0},{2,3},{3,2},{4,5},{5,4},{6,7},{7,6}} | collective-permute-start | bytes 9437192 | tf_op jit(solution)/shard_map/ppermute | solution.py:315
  266.8 206.9 %collective-permute-start.13 = (bf16[256,6144]{1,0:T(8,128)(2,1)S(1)}, bf16[256,6144]{1,0:T(8,128)(2,1)}, u32[]{:S(2)}, u32[]{:S(2)}) collective-permute-start(bf16[256,6144]{1,0:T(8,128)(2,1)S(1)} %collective-permute-done.10.refs_1_), channel_id=1, source_target_pairs={{0,2},{1,3},{2,0},{3,1},{4,6},{5,7},{6,4},{7,5}} | collective-permute-start | bytes 9437192 | tf_op jit(solution)/shard_map/ppermute | solution.py:315
  430.8 199.1 %collective-permute-start.19 = (bf16[256,6144]{1,0:T(8,128)(2,1)}, bf16[256,6144]{1,0:T(8,128)(2,1)}, u32[]{:S(2)}, u32[]{:S(2)}) collective-permute-start(bf16[256,6144]{1,0:T(8,128)(2,1)} %collective-permute-done.11.refs_6_), channel_id=1, source_target_pairs={{0,1},{1,0},{2,3},{3,2},{4,5},{5,4},{6,7},{7,6}} | collective-permute-start | bytes 9437192 | tf_op jit(solution)/shard_map/ppermute | solution.py:315
  473.7 155.6 %collective-permute-start.15 = (bf16[256,6144]{1,0:T(8,128)(2,1)}, bf16[256,6144]{1,0:T(8,128)(2,1)}, u32[]{:S(2)}, u32[]{:S(2)}) collective-permute-start(bf16[256,6144]{1,0:T(8,128)(2,1)} %collective-permute-done.12.refs_2_), channel_id=1, source_target_pairs={{0,2},{1,3},{2,0},{3,1},{4,6},{5,7},{6,4},{7,5}} | collective-permute-start | bytes 9437192 | tf_op jit(solution)/shard_map/ppermute | solution.py:315
  629.3 11.0 %collective-permute-start.18 = (bf16[256,6144]{1,0:T(8,128)(2,1)}, bf16[256,6144]{1,0:T(8,128)(2,1)}, u32[]{:S(2)}, u32[]{:S(2)}) collective-permute-start(bf16[256,6144]{1,0:T(8,128)(2,1)} %collective-permute-done.12.refs_2_), channel_id=1, source_target_pairs={{0,1},{1,0},{2,3},{3,2},{4,5},{5,4},{6,7},{7,6}} | collective-permute-start | bytes 9437192 | tf_op jit(solution)/shard_map/ppermute | solution.py:315
  629.4 10.5 %collective-permute-start.20 = (bf16[256,6144]{1,0:T(8,128)(2,1)}, bf16[256,6144]{1,0:T(8,128)(2,1)}, u32[]{:S(2)}, u32[]{:S(2)}) collective-permute-start(bf16[256,6144]{1,0:T(8,128)(2,1)} %collective-permute-done.13.refs_7_), channel_id=1, source_target_pairs={{0,1},{1,0},{2,3},{3,2},{4,5},{5,4},{6,7},{7,6}} | collective-permute-start | bytes 9437192 | tf_op jit(solution)/shard_map/ppermute | solution.py:315
  629.9 14.5 %collective-permute-start.21 = (bf16[256,6144]{1,0:T(8,128)(2,1)}, bf16[256,6144]{1,0:T(8,128)(2,1)}, u32[]{:S(2)}, u32[]{:S(2)}) collective-permute-start(bf16[256,6144]{1,0:T(8,128)(2,1)} %collective-permute-done.15.refs_8_), channel_id=1, source_target_pairs={{0,1},{1,0},{2,3},{3,2},{4,5},{5,4},{6,7},{7,6}} | collective-permute-start | bytes 9437192 | tf_op jit(solution)/shard_map/ppermute | solution.py:315
  629.9 37.6 %collective-permute-start.23 = (bf16[256,3072]{1,0:T(8,128)(2,1)}, bf16[256,3072]{1,0:T(8,128)(2,1)}, u32[]{:S(2)}, u32[]{:S(2)}) collective-permute-start(bf16[256,3072]{1,0:T(8,128)(2,1)} %shard_map.113.refs_1_), channel_id=1, source_target_pairs={{0,4},{4,0},{1,5},{5,1},{2,6},{6,2},{3,7},{7,3}} | collective-permute-start | bytes 4718600 | tf_op jit(solution)/shard_map/ppermute | solution.py:319
  634.7 66.4 %collective-permute-start.22 = (bf16[256,3072]{1,0:T(8,128)(2,1)}, bf16[256,3072]{1,0:T(8,128)(2,1)S(1)}, u32[]{:S(2)}, u32[]{:S(2)}) collective-permute-start(bf16[256,3072]{1,0:T(8,128)(2,1)} %shard_map.114.refs_2_), channel_id=1, source_target_pairs={{0,4},{4,0},{1,5},{5,1},{2,6},{6,2},{3,7},{7,3}} | collective-permute-start | bytes 4718600 | tf_op jit(solution)/shard_map/ppermute | solution.py:319
  639.8 94.5 %collective-permute-start.14 = (bf16[256,3072]{1,0:T(8,128)(2,1)}, bf16[256,3072]{1,0:T(8,128)(2,1)S(1)}, u32[]{:S(2)}, u32[]{:S(2)}) collective-permute-start(bf16[256,3072]{1,0:T(8,128)(2,1)} %shard_map.115.refs_3_), channel_id=1, source_target_pairs={{0,4},{4,0},{1,5},{5,1},{2,6},{6,2},{3,7},{7,3}} | collective-permute-start | bytes 4718600 | tf_op jit(solution)/shard_map/ppermute | solution.py:319
  701.1 1.2 copy-start.4
  734.3 1.2 copy-start.3
  735.5 21.8 %copy-start.1 = (f32[1024,64]{0,1:T(8,128)S(1)}, f32[1024,64]{0,1:T(8,128)}, u32[]{:S(2)}) copy-start(f32[1024,64]{0,1:T(8,128)} %param.12) | copy-start | bytes 786436

commit v2 on v1

v2 whole, which is shorter than its diff:
```python
import functools

import jax
import jax.numpy as jnp
import numpy as np
from jax import lax
from jax.experimental import pallas as pl
from jax.experimental.pallas import tpu as pltpu
from jax.sharding import PartitionSpec as P


EPS = 1.5625e-07
MASK_VALUE = -1e30
F32 = jnp.float32
BF16 = jnp.bfloat16
LOG2E = 1.4426950408889634
HD = 128
VLIM = 60 * 1024 * 1024


def cost(flops, nbytes):
    return pl.CostEstimate(flops=int(flops), bytes_accessed=int(nbytes), transcendentals=0)


def dot(a, b):
    return jnp.dot(a, b, preferred_element_type=F32)


def norm_kernel(x_ref, g_ref, h_ref):
    x = x_ref[...].astype(F32)
    inv = lax.rsqrt(jnp.mean(x * x, axis=-1, keepdims=True) + EPS)
    h_ref[...] = (x * inv * g_ref[...].astype(F32)).astype(BF16)


def norm(x, g):
    rows, d = x.shape
    rb = 128
    return pl.pallas_call(
        norm_kernel,
        grid=(rows // rb,),
        in_specs=[pl.BlockSpec((rb, d), lambda i: (i, 0)), pl.BlockSpec((1, d), lambda i: (0, 0))],
        out_specs=pl.BlockSpec((rb, d), lambda i: (i, 0)),
        out_shape=jax.ShapeDtypeStruct((rows, d), BF16),
        cost_estimate=cost(rows * d * 80, rows * d * 4),
        name="norm",
    )(x, g.reshape(1, d))


def rotate(v, cos_e, sin_e):
    lane = lax.broadcasted_iota(jnp.int32, v.shape, 1)
    swapped = jnp.where(lane % 2 == 0, pltpu.roll(v, HD - 1, 1), pltpu.roll(v, 1, 1))
    return jnp.where(lane < HD // 2, v * cos_e + swapped * sin_e, v)


MB = 512


def kv_kernel(groups, h_ref, w_ref, b_ref, c_ref, s_ref, k_ref, v_ref, vt_ref, q_ref):
    bias = b_ref[0].astype(F32)
    first = pl.program_id(0) < groups

    @pl.loop(0, h_ref.shape[0] // MB)
    def _(m):
        r = pl.ds(pl.multiple_of(m * MB, MB), MB)
        a = dot(h_ref[r, :], w_ref[...]) + bias
        left = rotate(a[:, :HD], c_ref[r, :], s_ref[r, :]).astype(BF16)

        @pl.when(first)
        def _():
            k_ref[r, :] = left
            v = a[:, HD:].astype(BF16)
            v_ref[r, :] = v
            vt_ref[:, r] = v.T

        @pl.when(jnp.logical_not(first))
        def _():
            q_ref[r, :HD] = left
            q_ref[r, HD:] = rotate(a[:, HD:], c_ref[r, :], s_ref[r, :]).astype(BF16)


def q_kernel(h_ref, w_ref, b_ref, c_ref, s_ref, q_ref):
    bias = b_ref[0].astype(F32)

    @pl.loop(0, h_ref.shape[0] // MB)
    def _(m):
        r = pl.ds(pl.multiple_of(m * MB, MB), MB)
        a = dot(h_ref[r, :], w_ref[...]) + bias
        q_ref[r, :HD] = rotate(a[:, :HD], c_ref[r, :], s_ref[r, :]).astype(BF16)
        q_ref[r, HD:] = rotate(a[:, HD:], c_ref[r, :], s_ref[r, :]).astype(BF16)


def proj_specs(rows, d, col):
    whole = lambda i: (0, 0)
    return [
        pl.BlockSpec((rows, d), whole),
        pl.BlockSpec((d, 2 * HD), lambda i: (0, col(i))),
        pl.BlockSpec((1, 1, 2 * HD), lambda i: (col(i), 0, 0)),
        pl.BlockSpec((rows, HD), whole),
        pl.BlockSpec((rows, HD), whole),
    ]


def project_kv(h, w, b, ce, se, groups):
    rows, d = h.shape
    per = w.shape[1] // (2 * HD * groups)
    nq = per - 1
    steps = groups + nq
    col = lambda i: jnp.where(i < groups, i * per + nq, i - groups + (groups - 1) * per)
    at = lambda i: jnp.minimum(i, groups - 1)
    return pl.pallas_call(
        functools.partial(kv_kernel, groups),
        grid=(steps,),
        in_specs=proj_specs(rows, d, col),
        out_specs=[
            pl.BlockSpec((rows, HD), lambda i: (0, at(i))),
            pl.BlockSpec((rows, HD), lambda i: (0, at(i))),
            pl.BlockSpec((HD, rows), lambda i: (at(i), 0)),
            pl.BlockSpec((rows, 2 * HD), lambda i: (0, jnp.maximum(i - groups, 0))),
        ],
        out_shape=[
            jax.ShapeDtypeStruct((rows, groups * HD), BF16),
            jax.ShapeDtypeStruct((rows, groups * HD), BF16),
            jax.ShapeDtypeStruct((groups * HD, rows), BF16),
            jax.ShapeDtypeStruct((rows, nq * 2 * HD), BF16),
        ],
        compiler_params=pltpu.CompilerParams(vmem_limit_bytes=VLIM),
        cost_estimate=cost(2 * rows * d * steps * 2 * HD, d * steps * 4 * HD + rows * d * 2),
        name="project_kv",
    )(h, w, b, ce, se)


def project_q(h, w, b, ce, se, groups):
    rows, d = h.shape
    per = w.shape[1] // (2 * HD * groups)
    nq = per - 1
    steps = (groups - 1) * nq
    col = lambda i: (i // nq) * per + i % nq
    return pl.pallas_call(
        q_kernel,
        grid=(steps,),
        in_specs=proj_specs(rows, d, col),
        out_specs=pl.BlockSpec((rows, 2 * HD), lambda i: (0, i)),
        out_shape=jax.ShapeDtypeStruct((rows, steps * 2 * HD), BF16),
        compiler_params=pltpu.CompilerParams(vmem_limit_bytes=VLIM),
        cost_estimate=cost(2 * rows * d * steps * 2 * HD, d * steps * 4 * HD + rows * d * 2),
        name="project_q",
    )(h, w, b, ce, se)


QB = 256
KB = 1024


def attn_kernel(chunk, remotes, group, tok, me_ref, q_ref, ql_ref, *refs):
    nr = 1 if remotes else 0
    qr_ref = refs[0] if nr else None
    kc, vc, ko, vo, ks, vs, kx, vx, kz, vz = refs[nr:nr + 10]
    outs = refs[nr + 10:nr + 12 + nr]
    kbuf, vbuf, qt, sbuf, acc, mrun, lrun, obuf, sem = refs[nr + 12 + nr:]
    g = pl.program_id(0)
    groups = kbuf.shape[0]
    last = groups - 1
    me = me_ref[0]
    mirror = lax.bitwise_xor(me, 3)
    pieces = [(None, kc, vc), (0, ko, vo), (1, ks, vs), (2, kx, vx), (3, kz, vz)]

    def each_copy(gg, act):
        reach = jnp.maximum(me, mirror) if gg == last and remotes else me
        for rel, kp, vp in pieces:
            n = kp.shape[0]
            src = None if rel is None else lax.bitwise_xor(me, rel)
            at = 0 if rel is None else pl.multiple_of(kc.shape[0] + src * tok, tok)

            def go(kp=kp, vp=vp, n=n, at=at):
                act(pltpu.make_async_copy(kp.at[:, pl.ds(gg * HD, HD)], kbuf.at[gg, pl.ds(at, n), :], sem.at[gg]))
                act(pltpu.make_async_copy(vp.at[pl.ds(gg * HD, HD), :], vbuf.at[gg, :, pl.ds(at, n)], sem.at[gg]))

            if rel in (None, 0):
                go()
            else:
                pl.when(src <= reach)(go)

    @pl.when(g == 0)
    def _():
        for gg in range(groups):
            each_copy(gg, lambda c: c.start())

    for gg in range(groups):
        @pl.when(g == gg)
        def _(gg=gg):
            each_copy(gg, lambda c: c.wait())

    def load_q(ref):
        for h in range(group):
            qt[h] = ref[:, h * HD:(h + 1) * HD].T

    pl.when(g < last)(lambda: load_q(q_ref))
    pl.when(g == last)(lambda: load_q(ql_ref))
    if remotes:
        pl.when(g > last)(lambda: load_q(qr_ref))

    conv = LOG2E * HD ** -0.5
    kvg = jnp.minimum(g, last)

    def step(at, n, mask):
        k = kbuf[kvg, pl.ds(at, n), :]
        vt = vbuf[kvg, :, pl.ds(at, n)]
        sbuf[0, :n] = dot(k, qt[0])
        for h in range(group):
            if h + 1 < group:
                sbuf[(h + 1) % 2, :n] = dot(k, qt[h + 1])
            s = sbuf[h % 2, :n]
            if mask is not None:
                s = jnp.where(mask, s, MASK_VALUE)
            m_old = mrun[h]
            m_new = jnp.maximum(m_old, jnp.max(s, axis=0, keepdims=True))
            p = jnp.exp2(s * conv - m_new * conv)
            alpha = jnp.exp2((m_old - m_new) * conv)
            mrun[h] = m_new
            lrun[h] = lrun[h] * alpha + p.reshape(n // 8, 8, QB).sum(axis=0)
            acc[h] = acc[h] * alpha + dot(vt, p.astype(BF16))

    @pl.when((me < 2) | (g < last))
    def _():
        acc[...] = jnp.zeros_like(acc)
        lrun[...] = jnp.zeros_like(lrun)
        mrun[...] = jnp.full_like(mrun, MASK_VALUE)

        nfull = (kc.shape[0] + jnp.where(g > last, mirror, me) * tok) // KB

        @pl.loop(0, nfull)
        def _(kb):
            step(pl.multiple_of(kb * KB, KB), KB, None)

        def finish(c):
            tail = (c + 1) * QB
            key = lax.broadcasted_iota(jnp.int32, (tail, QB), 0)
            row = lax.broadcasted_iota(jnp.int32, (tail, QB), 1)
            step(pl.multiple_of(nfull * KB, KB), tail, key <= row + c * QB)

        others = [(i, c) for i, c in enumerate(remotes) if c != chunk]
        same = g <= last
        for i, c in enumerate(remotes):
            if c == chunk:
                same = same | (g == groups + i)
        if others:
            pl.when(same)(lambda: finish(chunk))
            for i, c in others:
                pl.when(g == groups + i)(lambda c=c: finish(c))
        else:
            finish(chunk)

        for h in range(group):
            total = jnp.sum(lrun[h], axis=0, keepdims=True)
            obuf[:, h * HD:(h + 1) * HD] = (acc[h] / total).T.astype(BF16)

        def put(ref):
            ref[...] = obuf[...]

        pl.when(g < last)(lambda: put(outs[0]))
        pl.when(g == last)(lambda: put(outs[1]))
        if remotes:
            pl.when(g > last)(lambda: put(outs[2]))


def attend(chunk, remotes, me, q, ql, qr, pieces, group):
    tok = q.shape[0]
    gw = group * HD
    groups = q.shape[1] // gw + 1
    last = groups - 1
    ncache = pieces[0].shape[0]
    total = ncache + 4 * tok
    anyspec = pl.BlockSpec(memory_space=pl.ANY)
    in_specs = [
        pl.BlockSpec((QB, gw), lambda g, me: (chunk, jnp.minimum(g, last - 1))),
        pl.BlockSpec((QB, gw), lambda g, me: (chunk, 0)),
    ]
    out_specs = [
        pl.BlockSpec((QB, gw), lambda g, me: (0, jnp.minimum(g, last - 1))),
        pl.BlockSpec((QB, gw), lambda g, me: (0, 0)),
    ]
    out_shape = [jax.ShapeDtypeStruct((QB, last * gw), BF16), jax.ShapeDtypeStruct((QB, gw), BF16)]
    args = [q, ql]
    if remotes:
        nrem = len(remotes)
        pos = lambda g: jnp.clip(g - groups, 0, nrem - 1)
        in_specs.append(pl.BlockSpec((QB, gw), lambda g, me: (remotes[0] + pos(g), 0)))
        out_specs.append(pl.BlockSpec((QB, gw), lambda g, me: (pos(g), 0)))
        out_shape.append(jax.ShapeDtypeStruct((QB * nrem, gw), BF16))
        args.append(qr)
    return pl.pallas_call(
        functools.partial(attn_kernel, chunk, remotes, group, tok),
        grid_spec=pltpu.PrefetchScalarGridSpec(
            num_scalar_prefetch=1,
            grid=(groups + len(remotes),),
            in_specs=in_specs + [anyspec] * 10,
            out_specs=out_specs,
            scratch_shapes=[
                pltpu.VMEM((groups, total, HD), BF16),
                pltpu.VMEM((groups, HD, total), BF16),
                pltpu.VMEM((group, HD, QB), BF16),
                pltpu.VMEM((2, KB, QB), F32),
                pltpu.VMEM((group, HD, QB), F32),
                pltpu.VMEM((group, 1, QB), F32),
                pltpu.VMEM((group, 8, QB), F32),
                pltpu.VMEM((QB, gw), BF16),
                pltpu.SemaphoreType.DMA((groups,)),
            ],
        ),
        out_shape=out_shape,
        compiler_params=pltpu.CompilerParams(vmem_limit_bytes=VLIM),
        cost_estimate=cost(40e9, 12e6),
    )(me, *args, *pieces)


def gather_rows(pieces, obuf, sem):
    @pl.when(pl.program_id(0) == 0)
    def _():
        copies = [pltpu.make_async_copy(c, obuf.at[pl.ds(r, c.shape[0]), pl.ds(w, c.shape[1])], sem.at[i])
                  for i, (r, w, c) in enumerate(pieces)]
        for c in copies:
            c.start()
        for c in copies:
            c.wait()


def layout(chunks):
    places = []
    for i, (a, b) in enumerate(chunks):
        places += [(i * a.shape[0], 0), (i * a.shape[0], a.shape[1])]
    return places


def own_kernel(places, x_ref, w_ref, *refs):
    n = len(places)
    y_ref, obuf, sem = refs[n:]
    gather_rows([(r, c, ref) for (r, c), ref in zip(places, refs[:n])], obuf, sem)

    @pl.loop(0, obuf.shape[0] // MB)
    def _(m):
        r = pl.ds(pl.multiple_of(m * MB, MB), MB)
        y_ref[r, :] = x_ref[r, :].astype(F32) + dot(obuf[r, :], w_ref[...])


def own_part(x, w, chunks):
    rows, d = x.shape
    inner = w.shape[0]
    nb = 512
    places = layout(chunks)
    return pl.pallas_call(
        functools.partial(own_kernel, places),
        grid=(d // nb,),
        in_specs=[
            pl.BlockSpec((rows, nb), lambda i: (0, i)),
            pl.BlockSpec((inner, nb), lambda i: (0, i)),
        ] + [pl.BlockSpec(memory_space=pl.ANY)] * len(places),
        out_specs=pl.BlockSpec((rows, nb), lambda i: (0, i)),
        out_shape=jax.ShapeDtypeStruct((rows, d), F32),
        scratch_shapes=[pltpu.VMEM((rows, inner), BF16), pltpu.SemaphoreType.DMA((len(places),))],
        compiler_params=pltpu.CompilerParams(vmem_limit_bytes=VLIM),
        cost_estimate=cost(2 * rows * inner * d, rows * d * 6 + inner * d * 2),
        name="own_part",
    )(x, w, *[p for c in chunks for p in c])


def other_kernel(nper, places, me_ref, a_ref, *refs):
    me = me_ref[0]
    nw, n = 4 * nper, len(places)
    ws, pieces = refs[:nw], refs[nw:nw + n]
    y_ref, obuf, sem = refs[-3:]
    gather_rows([(r, c, ref) for (r, c), ref in zip(places, pieces)], obuf, sem)
    wr = ws[0].shape[0]
    total = a_ref[...]
    for i in range(nw):
        quarter = lax.bitwise_xor(me, i // nper)
        at = pl.multiple_of(quarter * (nper * wr) + (i % nper) * wr, wr)
        total = total + dot(obuf[:, pl.ds(at, wr)], ws[i][...])
    y_ref[...] = total.astype(BF16)


def other_part(call, me, chunks, partial, ws, y):
    places = layout(chunks)
    rows = len(chunks) * chunks[0][0].shape[0]
    d = partial.shape[1]
    nb = 1024
    wr = ws[0].shape[0]
    extra = [] if y is None else [y]
    return pl.pallas_call(
        functools.partial(other_kernel, len(ws) // 4, places),
        grid_spec=pltpu.PrefetchScalarGridSpec(
            num_scalar_prefetch=1,
            grid=(d // nb,),
            in_specs=[pl.BlockSpec((rows, nb), lambda i, me: (call, i))]
            + [pl.BlockSpec((wr, nb), lambda i, me: (0, i))] * len(ws)
            + [pl.BlockSpec(memory_space=pl.ANY)] * (len(places) + len(extra)),
            out_specs=pl.BlockSpec((rows, nb), lambda i, me: (call, i)),
            scratch_shapes=[pltpu.VMEM((rows, wr * len(ws)), BF16), pltpu.SemaphoreType.DMA((len(places),))],
        ),
        out_shape=jax.ShapeDtypeStruct(partial.shape, BF16),
        input_output_aliases={} if y is None else {2 + len(ws) + len(places): 0},
        compiler_params=pltpu.CompilerParams(vmem_limit_bytes=VLIM),
        cost_estimate=cost(2 * rows * wr * len(ws) * d, rows * d * 6 + wr * len(ws) * d * 2),
    )(me, partial, *ws, *[p for c in chunks for p in c], *extra)


def cp_send(v, rel):
    return lax.ppermute(v, 'cp', [(i, i ^ rel) for i in range(4)])


def cp_move(v, pairs):
    return lax.ppermute(v, 'cp', pairs)


def tp_send(v):
    return lax.ppermute(v, 'tp', [(0, 1), (1, 0)])


def spread_matrices(half, hd):
    out = np.zeros((2 * half, 2 * hd), np.float32)
    for lane in range(2 * half):
        out[lane // 2, lane] = 1.0
        out[half + lane // 2, hd + lane] = 1.0 if lane % 2 else -1.0
    return out


def block(x, k_cache, v_cache, rope_table, norm_gain, w_qkv, b_qkv, w_out):
    tok, d = x.shape
    ncache, groups, hd = k_cache.shape
    group = w_qkv.shape[1] // (groups * hd) - 2
    cp = lax.axis_index('cp')
    me = cp.astype(jnp.int32).reshape(1)
    bar = lax.optimization_barrier

    nper = 3
    wr = w_out.shape[0] // (4 * nper)
    w_parts = [lax.dynamic_slice(w_out, (cp * (nper * wr) + i * wr, 0), (wr, d)) for i in range(nper)]
    wy = [tp_send(p) for p in w_parts]

    cache = jnp.concatenate([k_cache.reshape(ncache, groups * hd), v_cache.reshape(ncache, groups * hd)], axis=1)
    caches = jnp.concatenate([cache] + [cp_send(cache, r) for r in (1, 2, 3)], axis=0)
    kc = caches[:, :groups * hd]
    vc = caches[:, groups * hd:].T

    half = rope_table.shape[1] // 2
    spread = jnp.dot(rope_table, spread_matrices(half, hd), precision=lax.Precision.HIGHEST)
    ce, se = spread[:, :hd], spread[:, hd:]
    bias = b_qkv.reshape(-1, 1, 2 * hd)

    h = norm(x, norm_gain)
    k, v, vt, ql = project_kv(h, w_qkv, bias, ce, se, groups)
    ks, vs = cp_send(k, 1), cp_send(vt, 1)
    kx, vx = cp_send(k, 2), cp_send(vt, 2)
    qr = cp_move(ql, [(2, 1), (3, 0)])
    q = project_q(h, w_qkv, bias, ce, se, groups)
    (q, kx, vx, wy[0]) = bar((q, kx, vx, wy[0]))
    kz, vz = cp_send(kx, 1), cp_send(vx, 1)
    pieces = [kc, vc, k, vt, ks, vs, kx, vx, kz, vz]

    wx, wd, wz = [None] * nper, [None] * nper, [None] * nper

    def forward(i):
        wx[i], wd[i] = cp_send(wy[i], 2), cp_send(wy[i], 1)

    def relay(i):
        wz[i] = cp_send(wx[i], 1)

    forward(0)
    nchunk = tok // QB
    remotes = [(0,), (1,), (2, 3), ()]
    mine, theirs = [], []
    lasts, back, other_last = [None] * nchunk, [None] * nchunk, [None] * nchunk

    def settle(c):
        lasts[c] = jnp.where(cp >= 2, back[c], lasts[c])
        other_last[c] = tp_send(lasts[c])

    for chunk in range(nchunk):
        o, lasts[chunk], *rem = attend(chunk, remotes[chunk], me, q, ql, qr, pieces, group)
        if chunk == 0:
            (o, q) = bar((o, q))
        elif chunk == 1:
            (o, q, wy[1], wx[0], back[0]) = bar((o, q, wy[1], wx[0], back[0]))
            forward(1)
            relay(0)
            settle(0)
        elif chunk == 2:
            (o, q, back[1]) = bar((o, q, back[1]))
            settle(1)
        else:
            (o, q, wy[2], wx[1], back[2], back[3]) = bar((o, q, wy[2], wx[1], back[2], back[3]))
            settle(2)
            settle(3)
            forward(2)
            relay(1)
        if rem:
            got = cp_move(rem[0], [(0, 3), (1, 2)])
            for i, c in enumerate(remotes[chunk]):
                back[c] = got[i * QB:(i + 1) * QB]
        mine.append(o)
        theirs.append(tp_send(o))

    partial = own_part(x, w_out, list(zip(mine, lasts)))
    (partial, wx[2]) = bar((partial, wx[2]))
    relay(2)
    ws = wy + wd + wx + wz
    y = None
    for call in range(nchunk // 2):
        chunks = [(theirs[c], other_last[c]) for c in (2 * call, 2 * call + 1)]
        y = other_part(call, me, chunks, partial, ws, y)
    return y, k.reshape(tok, groups, hd), v.reshape(tok, groups, hd)


def solution(mesh):
    row_spec = P(('dp', 'cp'), None)
    cache_spec = P(('dp', 'cp'), 'tp', None)
    return jax.shard_map(block, mesh=mesh, in_specs=(row_spec, cache_spec, cache_spec, row_spec, P(None), P(None, 'tp'), P('tp'), P('tp', None)), out_specs=(row_spec, cache_spec, cache_spec), check_vma=False)
```

time: 758 us -> 660 us (0.87)
  starting transfers between devices: 219 us -> 51.1 us
  waiting for transfers between devices: 120 us -> 243 us
  Pallas kernels: 390 us -> 327 us
    ppermute x18, starting transfers between devices: 211 us -> 17.2 us  [cp_send(): return lax.ppermute(v, 'cp', [(i, i ^ rel) for i in range(4)])]
    ppermute x18, waiting for transfers between devices: 38.4 us -> 158 us  [cp_send(): return lax.ppermute(v, 'cp', [(i, i ^ rel) for i in range(4)])]
    pallas_call x11 -> x9, Pallas kernels: 376 us -> 313 us  [the longest x4 126 us: attend(): pl.pallas_call(functools.partial(attn_kernel, chunk, remotes, group, tok)...]
    ppermute x0 -> x4, starting transfers between devices: none -> 21 us  [cp_move(): return lax.ppermute(v, 'cp', pairs)]
    ppermute x7 -> x11, waiting for transfers between devices: 82 us -> 84.9 us  [tp_send(): return lax.ppermute(v, 'tp', [(0, 1), (1, 0)])]
  transfers between devices with their start and end apart: 25 -> 33, of which waited for: 8 -> 11; matrix products, arithmetic and copies ran while one was open for 2% -> 5% of each run, Pallas kernels for 44% -> 38%
where the time goes in v2:
time: 660 us; the launch traced here: 659 us
  Pallas kernels  327 us (50%)
  waiting for transfers between devices  243 us (37%)
  starting transfers between devices  51.1 us (8%)
  local copies, waits for them, and re-layouts  24.5 us (4%)
  other arithmetic  10.6 us (2%)
    ppermute x18, waiting for transfers between devices, cp_send(): return lax.ppermute(v, 'cp', [(i, i ^ rel) for i in range(4)])  158 us
    pallas_call x4, Pallas kernels, attend(): pl.pallas_call(functools.partial(attn_kernel, chunk, remotes, group, tok)...  126 us
    ppermute x11, waiting for transfers between devices, tp_send(): return lax.ppermute(v, 'tp', [(0, 1), (1, 0)])  84.9 us
    pallas_call x2, Pallas kernels, other_part(): pl.pallas_call(functools.partial(other_kernel, len(ws) // 4, places), gri...  58.7 us
    pallas_call x1, Pallas kernels, own_part(): pl.pallas_call(functools.partial(own_kernel, places), grid=(d // nb,), in...  50.2 us
    pallas_call x1, Pallas kernels, project_q(): pl.pallas_call(q_kernel, grid=(steps,), in_specs=proj_specs(rows, d, col)...  43 us
    pallas_call x1, Pallas kernels, project_kv(): pl.pallas_call(functools.partial(kv_kernel, groups), grid=(steps,), in_sp...  35.4 us
    ppermute x4, starting transfers between devices, cp_move(): return lax.ppermute(v, 'cp', pairs)  21 us
  transfers between devices with their start and end apart: 33, of which 11 were waited for; matrix products, arithmetic and copies ran while one was open for 5% of the time, Pallas kernels for 38%

profile of v2, /device:TPU:0, one launch (start us, length us, event | category | flops | bytes accessed | tf_op | source)
XLA Modules:
  0.0 658.9 jit_solution(16336261246707995385)
XLA Ops:
  6.3 13.9 %norm.1.h_ref = bf16[1024,6144]{1,0:T(8,128)(2,1)} custom-call(bf16[1024,6144]{1,0:T(8,128)(2,1)} %x_ref.3, bf16[1,6144]{1,0:T(2,128)(2,1)} %reshape.28.g_ref), custom_call_target="tpu_custom_call" | custom-call | flops 503316480 | bytes 25165824 | tf_op jit(solution)/shard_map/norm/pallas_call | solution.py:38
  20.2 35.4 %project_kv.1 = (bf16[1024,512]{1,0:T(8,128)(2,1)}, bf16[1024,512]{1,0:T(8,128)(2,1)}, bf16[512,1024]{1,0:T(8,128)(2,1)}, bf16[1024,768]{1,0:T(8,128)(2,1)}) custom-call(bf16[1024,6144]{1,0:T(8,128)(2,1)} %norm.1.h_ref, bf16[6144,4096]{1,0:T(8,128)(2,1)} %w_ref.4, bf16[16,1,256]{2,1,0:T(2,128)(2,1)} %reshape.34.b_ref, f32[1024,128]{1,0:T(8,128)} %get-tuple-element.81.c_ref, ...), custom_call_target="tpu_custom_call" | custom-call | flops 22548578304 | bytes 34603008 | tf_op jit(solution)/shard_map/project_kv/pallas_call | solution.py:110
  55.6 3.3 collective-permute-start.1
  59.0 7.8 %constant_dynamic-slice_fusion = (bf16[256,6144]{1,0:T(8,128)(2,1)}, bf16[256,6144]{1,0:T(8,128)(2,1)}, bf16[256,6144]{1,0:T(8,128)(2,1)}) fusion(bf16[3072,6144]{1,0:T(8,128)(2,1)} %w_ref.5, s32[]{:T(128)S(6)} %select_n.34, s32[]{:T(128)S(6)} %select_n.31, s32[]{:T(128)S(6)} %select_n.29), kind=kLoop, calls=%fused_computation.8 | loop fusion | bytes 18874380 | tf_op jit(solution)/shard_map/dynamic_slice | solution.py:436
  74.9 8.4 %collective-permute-done.1.refs_8_.refs_7_ = bf16[512,1024]{1,0:T(8,128)(2,1)} collective-permute-done((bf16[512,1024]{1,0:T(8,128)(2,1)}, bf16[512,1024]{1,0:T(8,128)(2,1)}, u32[]{:S(2)}, u32[]{:S(2)}) %collective-permute-start.1) | collective-permute-done | bytes 1048608 | tf_op jit(solution)/shard_map/ppermute | solution.py:407
  83.3 22.5 %collective-permute-done.refs_7_.refs_6_ = bf16[1024,512]{1,0:T(8,128)(2,1)} collective-permute-done((bf16[1024,512]{1,0:T(8,128)(2,1)}, bf16[1024,512]{1,0:T(8,128)(2,1)}, u32[]{:S(2)}, u32[]{:S(2)}) %collective-permute-start) | collective-permute-done | bytes 1048608 | tf_op jit(solution)/shard_map/ppermute | solution.py:407
  107.3 43.0 %project_q.1.q_ref = bf16[1024,2304]{1,0:T(8,128)(2,1)} custom-call(bf16[1024,6144]{1,0:T(8,128)(2,1)} %norm.1.h_ref, bf16[6144,4096]{1,0:T(8,128)(2,1)} %w_ref.4, bf16[16,1,256]{2,1,0:T(2,128)(2,1)} %reshape.34.b_ref, f32[1024,128]{1,0:T(8,128)} %get-tuple-element.81.c_ref, f32[1024,128]{1,0:T(8,128)} %get-tuple-element.80.s_ref), custom_call_target="tpu_custom_call" | custom-call | flops 28991029248 | bytes 40894464 | tf_op jit(solution)/shard_map/project_q/pallas_call | solution.py:138
  151.4 3.4 pad_maximum_fusion
  156.3 2.3 copy.25.refs_1_.refs_0_
  160.6 3.2 collective-permute-start.12
  163.8 28.4 %shard_map.112 = (bf16[256,2304]{1,0:T(8,128)(2,1)}, bf16[256,768]{1,0:T(8,128)(2,1)}, bf16[256,768]{1,0:T(8,128)(2,1)}) custom-call(s32[1]{0:T(128)} %bitcast.me_ref, bf16[1024,2304]{1,0:T(8,128)(2,1)} %project_q.1.q_ref, bf16[1024,768]{1,0:T(8,128)(2,1)} %get-tuple-element.42.ql_ref, bf16[1024,768]{1,0:T(8,128)(2,1)} %collective-permute-done.3.refs_0_, ...), custom_call_target="tpu_custom_call" | custom-call | flops 40000000000 | bytes 12000000 | tf_op jit(solution)/shard_map/pallas_call | solution.py:291
  192.2 8.7 %collective-permute-start.13 = (bf16[256,768]{1,0:T(8,128)(2,1)}, bf16[256,768]{1,0:T(8,128)(2,1)S(1)}, u32[]{:S(2)}, u32[]{:S(2)}) collective-permute-start(bf16[256,768]{1,0:T(8,128)(2,1)} %get-tuple-element.50), channel_id=1, source_target_pairs={{0,3},{1,2},{4,7},{5,6}} | collective-permute-start | bytes 1179656 | tf_op jit(solution)/shard_map/ppermute | solution.py:411
  200.9 30.3 %shard_map.113 = (bf16[256,2304]{1,0:T(8,128)(2,1)}, bf16[256,768]{1,0:T(8,128)(2,1)}, bf16[256,768]{1,0:T(8,128)(2,1)}) custom-call(s32[1]{0:T(128)} %bitcast.me_ref, bf16[1024,2304]{1,0:T(8,128)(2,1)} %project_q.1.q_ref, bf16[1024,768]{1,0:T(8,128)(2,1)} %get-tuple-element.42.ql_ref, bf16[1024,768]{1,0:T(8,128)(2,1)} %collective-permute-done.3.refs_0_, ...), custom_call_target="tpu_custom_call" | custom-call | flops 40000000000 | bytes 12000000 | tf_op jit(solution)/shard_map/pallas_call | solution.py:291
  231.2 8.2 %collective-permute-start.14 = (bf16[256,768]{1,0:T(8,128)(2,1)}, bf16[256,768]{1,0:T(8,128)(2,1)}, u32[]{:S(2)}, u32[]{:S(2)}) collective-permute-start(bf16[256,768]{1,0:T(8,128)(2,1)} %get-tuple-element.56), channel_id=1, source_target_pairs={{0,3},{1,2},{4,7},{5,6}} | collective-permute-start | bytes 1179656 | tf_op jit(solution)/shard_map/ppermute | solution.py:411
  239.4 57.2 %collective-permute-done.11.refs_1_ = bf16[256,6144]{1,0:T(8,128)(2,1)} collective-permute-done((bf16[256,6144]{1,0:T(8,128)(2,1)}, bf16[256,6144]{1,0:T(8,128)(2,1)}, u32[]{:S(2)}, u32[]{:S(2)}) %collective-permute-start.11) | collective-permute-done | bytes 3145760 | tf_op jit(solution)/shard_map/ppermute | solution.py:415
  296.6 44.5 %shard_map.114 = (bf16[256,2304]{1,0:T(8,128)(2,1)}, bf16[256,768]{1,0:T(8,128)(2,1)}, bf16[512,768]{1,0:T(8,128)(2,1)}) custom-call(s32[1]{0:T(128)} %bitcast.me_ref, bf16[1024,2304]{1,0:T(8,128)(2,1)} %project_q.1.q_ref, bf16[1024,768]{1,0:T(8,128)(2,1)} %get-tuple-element.42.ql_ref, bf16[1024,768]{1,0:T(8,128)(2,1)} %collective-permute-done.3.refs_0_, ...), custom_call_target="tpu_custom_call" | custom-call | flops 40000000000 | bytes 12000000 | tf_op jit(solution)/shard_map/pallas_call | solution.py:291
  341.2 2.5 collective-permute-start.17
  343.7 22.5 %shard_map.115 = (bf16[256,2304]{1,0:T(8,128)(2,1)}, bf16[256,768]{1,0:T(8,128)(2,1)}) custom-call(s32[1]{0:T(128)} %bitcast.me_ref, bf16[1024,2304]{1,0:T(8,128)(2,1)} %project_q.1.q_ref, bf16[1024,768]{1,0:T(8,128)(2,1)} %get-tuple-element.42.ql_ref, bf16[1024,512]{1,0:T(8,128)(2,1)} %copy.25.refs_1_.refs_0_, ...), custom_call_target="tpu_custom_call" | custom-call | flops 40000000000 | bytes 12000000 | tf_op jit(solution)/shard_map/pallas_call | solution.py:291
  368.3 56.8 %collective-permute-done.16.refs_7_ = bf16[256,6144]{1,0:T(8,128)(2,1)} collective-permute-done((bf16[256,6144]{1,0:T(8,128)(2,1)}, bf16[256,6144]{1,0:T(8,128)(2,1)}, u32[]{:S(2)}, u32[]{:S(2)}) %collective-permute-start.16) | collective-permute-done | bytes 3145760 | tf_op jit(solution)/shard_map/ppermute | solution.py:407
  425.0 2.5 collective-permute-start.18
  427.5 2.9 collective-permute-start.19
  439.7 54.6 %collective-permute-done.18.refs_8_ = bf16[256,6144]{1,0:T(8,128)(2,1)} collective-permute-done((bf16[256,6144]{1,0:T(8,128)(2,1)}, bf16[256,6144]{1,0:T(8,128)(2,1)}, u32[]{:S(2)}, u32[]{:S(2)}) %collective-permute-start.18) | collective-permute-done | bytes 3145760 | tf_op jit(solution)/shard_map/ppermute | solution.py:407
  494.3 2.4 collective-permute-start.31
  496.7 50.2 %own_part.1.a_ref = f32[1024,6144]{1,0:T(8,128)} custom-call(bf16[1024,6144]{1,0:T(8,128)(2,1)} %x_ref.3, bf16[3072,6144]{1,0:T(8,128)(2,1)} %w_ref.5, bf16[256,2304]{1,0:T(8,128)(2,1)} %get-tuple-element.46.refs_0_, bf16[256,768]{1,0:T(8,128)(2,1)} %copy-done.10, bf16[256,2304]{1,0:T(8,128)(2,1)} %get-tuple-element.53.refs_2_, ...), custom_call_target="tpu_custom_call" | custom-call | flops 38654705664 | bytes 75497472 | tf_op jit(solution)/shard_map/own_part/pallas_call | solution.py:350
  554.0 4.7 collective-permute-done.22.refs_9_
  560.7 2.6 collective-permute-done.23.refs_10_
  563.6 4.2 collective-permute-done.21.refs_5_
  568.1 4.2 collective-permute-done.24.refs_11_
  572.3 29.3 %shard_map.116.refs_16_ = bf16[1024,6144]{1,0:T(8,128)(2,1)} custom-call(s32[1]{0:T(128)} %bitcast.me_ref, f32[1024,6144]{1,0:T(8,128)} %own_part.1.a_ref, bf16[256,6144]{1,0:T(8,128)(2,1)} %copy-done.2, bf16[256,6144]{1,0:T(8,128)(2,1)} %collective-permute-done.11.refs_1_, bf16[256,6144]{1,0:T(8,128)(2,1)} %collective-permute-done.15.refs_2_, ...), custom_call_target="tpu_custom_call" | custom-call | flops 19327352832 | bytes 56623104 | tf_op jit(solution)/shard_map/pallas_call | solution.py:388
  601.6 3.0 collective-permute-done.26.refs_13_
  604.7 24.7 %collective-permute-done.27.refs_14_ = bf16[256,2304]{1,0:T(8,128)(2,1)} collective-permute-done((bf16[256,2304]{1,0:T(8,128)(2,1)}, bf16[256,2304]{1,0:T(8,128)(2,1)}, u32[]{:S(2)}, u32[]{:S(2)}) %collective-permute-start.27) | collective-permute-done | bytes 1179680 | tf_op jit(solution)/shard_map/ppermute | solution.py:415
  629.3 29.3 %shard_map.117 = bf16[1024,6144]{1,0:T(8,128)(2,1)} custom-call(s32[1]{0:T(128)} %bitcast.me_ref, f32[1024,6144]{1,0:T(8,128)} %own_part.1.a_ref, bf16[256,6144]{1,0:T(8,128)(2,1)} %copy-done.2, bf16[256,6144]{1,0:T(8,128)(2,1)} %collective-permute-done.11.refs_1_, ...), custom_call_target="tpu_custom_call", output_to_operand_aliasing={{}: (18, {})} | custom-call | flops 19327352832 | bytes 56623104 | tf_op jit(solution)/shard_map/pallas_call | solution.py:388
  (84 shorter events, 41.1 us)
Async XLA Ops:
  55.6 27.6 %collective-permute-start.1 = (bf16[512,1024]{1,0:T(8,128)(2,1)}, bf16[512,1024]{1,0:T(8,128)(2,1)}, u32[]{:S(2)}, u32[]{:S(2)}) collective-permute-start(bf16[512,1024]{1,0:T(8,128)(2,1)} %get-tuple-element.40.refs_4_.refs_3_), channel_id=1, source_target_pairs={{0,2},{1,3},{2,0},{3,1},{4,6},{5,7},{6,4},{7,5}} | collective-permute-start | bytes 3145736 | tf_op jit(solution)/shard_map/ppermute | solution.py:407
  58.9 46.8 %collective-permute-start = (bf16[1024,512]{1,0:T(8,128)(2,1)}, bf16[1024,512]{1,0:T(8,128)(2,1)}, u32[]{:S(2)}, u32[]{:S(2)}) collective-permute-start(bf16[1024,512]{1,0:T(8,128)(2,1)} %get-tuple-element.39.refs_3_.refs_2_), channel_id=1, source_target_pairs={{0,2},{1,3},{2,0},{3,1},{4,6},{5,7},{6,4},{7,5}} | collective-permute-start | bytes 3145736 | tf_op jit(solution)/shard_map/ppermute | solution.py:407
  66.7 83.6 %collective-permute-start.2 = (bf16[256,6144]{1,0:T(8,128)(2,1)}, bf16[256,6144]{1,0:T(8,128)(2,1)S(1)}, u32[]{:S(2)}, u32[]{:S(2)}) collective-permute-start(bf16[256,6144]{1,0:T(8,128)(2,1)} %get-tuple-element.77), channel_id=1, source_target_pairs={{0,4},{4,0},{1,5},{5,1},{2,6},{6,2},{3,7},{7,3}} | collective-permute-start | bytes 9437192 | tf_op jit(solution)/shard_map/ppermute | solution.py:415
  73.4 77.0 %collective-permute-start.6 = (bf16[256,1024]{0,1:T(8,128)(2,1)}, bf16[256,1024]{0,1:T(8,128)(2,1)}, u32[]{:S(2)}, u32[]{:S(2)}) collective-permute-start(bf16[256,1024]{0,1:T(8,128)(2,1)} %pad_maximum_fusion.1), channel_id=1, source_target_pairs={{0,3},{1,2},{2,1},{3,0},{4,7},{5,6},{6,5},{7,4}} | collective-permute-start | bytes 1572872 | tf_op jit(solution)/shard_map/ppermute | solution.py:407
  73.5 77.4 %collective-permute-start.5 = (bf16[256,1024]{0,1:T(8,128)(2,1)}, bf16[256,1024]{0,1:T(8,128)(2,1)}, u32[]{:S(2)}, u32[]{:S(2)}) collective-permute-start(bf16[256,1024]{0,1:T(8,128)(2,1)} %pad_maximum_fusion.1), channel_id=1, source_target_pairs={{0,2},{1,3},{2,0},{3,1},{4,6},{5,7},{6,4},{7,5}} | collective-permute-start | bytes 1572872 | tf_op jit(solution)/shard_map/ppermute | solution.py:407
  83.3 67.7 %collective-permute-start.4 = (bf16[256,1024]{0,1:T(8,128)(2,1)}, bf16[256,1024]{0,1:T(8,128)(2,1)}, u32[]{:S(2)}, u32[]{:S(2)}) collective-permute-start(bf16[256,1024]{0,1:T(8,128)(2,1)} %pad_maximum_fusion.1), channel_id=1, source_target_pairs={{0,1},{1,0},{2,3},{3,2},{4,5},{5,4},{6,7},{7,6}} | collective-permute-start | bytes 1572872 | tf_op jit(solution)/shard_map/ppermute | solution.py:407
  105.7 54.9 %collective-permute-start.3 = (bf16[1024,768]{1,0:T(8,128)(2,1)}, bf16[1024,768]{1,0:T(8,128)(2,1)}, u32[]{:S(2)}, u32[]{:S(2)}) collective-permute-start(bf16[1024,768]{1,0:T(8,128)(2,1)} %get-tuple-element.42.ql_ref), channel_id=1, source_target_pairs={{2,1},{3,0},{6,5},{7,4}} | collective-permute-start | bytes 4718600 | tf_op jit(solution)/shard_map/ppermute | solution.py:411
  150.4 10.2 %collective-permute-start.7 = (bf16[1024,512]{1,0:T(8,128)(2,1)}, bf16[1024,512]{1,0:T(8,128)(2,1)}, u32[]{:S(2)}, u32[]{:S(2)}) collective-permute-start(bf16[1024,512]{1,0:T(8,128)(2,1)} %get-tuple-element.39.refs_3_.refs_2_), channel_id=1, source_target_pairs={{0,1},{1,0},{2,3},{3,2},{4,5},{5,4},{6,7},{7,6}} | collective-permute-start | bytes 3145736 | tf_op jit(solution)/shard_map/ppermute | solution.py:407
  150.9 13.0 %collective-permute-start.9 = (bf16[1024,512]{1,0:T(8,128)(2,1)}, bf16[1024,512]{1,0:T(8,128)(2,1)}, u32[]{:S(2)}, u32[]{:S(2)}) collective-permute-start(bf16[1024,512]{1,0:T(8,128)(2,1)} %collective-permute-done.refs_7_.refs_6_), channel_id=1, source_target_pairs={{0,1},{1,0},{2,3},{3,2},{4,5},{5,4},{6,7},{7,6}} | collective-permute-start | bytes 3145736 | tf_op jit(solution)/shard_map/ppermute | solution.py:407
  150.9 12.9 %collective-permute-start.10 = (bf16[512,1024]{1,0:T(8,128)(2,1)}, bf16[512,1024]{1,0:T(8,128)(2,1)}, u32[]{:S(2)}, u32[]{:S(2)}) collective-permute-start(bf16[512,1024]{1,0:T(8,128)(2,1)} %collective-permute-done.1.refs_8_.refs_7_), channel_id=1, source_target_pairs={{0,1},{1,0},{2,3},{3,2},{4,5},{5,4},{6,7},{7,6}} | collective-permute-start | bytes 3145736 | tf_op jit(solution)/shard_map/ppermute | solution.py:407
  158.5 209.7 %collective-permute-start.15 = (bf16[256,6144]{1,0:T(8,128)(2,1)}, bf16[256,6144]{1,0:T(8,128)(2,1)}, u32[]{:S(2)}, u32[]{:S(2)}) collective-permute-start(bf16[256,6144]{1,0:T(8,128)(2,1)} %get-tuple-element.75), channel_id=1, source_target_pairs={{0,4},{4,0},{1,5},{5,1},{2,6},{6,2},{3,7},{7,3}} | collective-permute-start | bytes 9437192 | tf_op jit(solution)/shard_map/ppermute | solution.py:415
  160.6 136.0 %collective-permute-start.11 = (bf16[256,6144]{1,0:T(8,128)(2,1)}, bf16[256,6144]{1,0:T(8,128)(2,1)}, u32[]{:S(2)}, u32[]{:S(2)}) collective-permute-start(bf16[256,6144]{1,0:T(8,128)(2,1)} %get-tuple-element.76), channel_id=1, source_target_pairs={{0,4},{4,0},{1,5},{5,1},{2,6},{6,2},{3,7},{7,3}} | collective-permute-start | bytes 9437192 | tf_op jit(solution)/shard_map/ppermute | solution.py:415
  160.6 136.0 %collective-permute-start.12 = (bf16[256,6144]{1,0:T(8,128)(2,1)S(1)}, bf16[256,6144]{1,0:T(8,128)(2,1)}, u32[]{:S(2)}, u32[]{:S(2)}) collective-permute-start(bf16[256,6144]{1,0:T(8,128)(2,1)S(1)} %collective-permute-done.2.refs_0_), channel_id=1, source_target_pairs={{0,2},{1,3},{2,0},{3,1},{4,6},{5,7},{6,4},{7,5}} | collective-permute-start | bytes 9437192 | tf_op jit(solution)/shard_map/ppermute | solution.py:407
  192.2 104.4 %collective-permute-start.13 = (bf16[256,768]{1,0:T(8,128)(2,1)}, bf16[256,768]{1,0:T(8,128)(2,1)S(1)}, u32[]{:S(2)}, u32[]{:S(2)}) collective-permute-start(bf16[256,768]{1,0:T(8,128)(2,1)} %get-tuple-element.50), channel_id=1, source_target_pairs={{0,3},{1,2},{4,7},{5,6}} | collective-permute-start | bytes 1179656 | tf_op jit(solution)/shard_map/ppermute | solution.py:411
  231.2 109.9 %collective-permute-start.14 = (bf16[256,768]{1,0:T(8,128)(2,1)}, bf16[256,768]{1,0:T(8,128)(2,1)}, u32[]{:S(2)}, u32[]{:S(2)}) collective-permute-start(bf16[256,768]{1,0:T(8,128)(2,1)} %get-tuple-element.56), channel_id=1, source_target_pairs={{0,3},{1,2},{4,7},{5,6}} | collective-permute-start | bytes 1179656 | tf_op jit(solution)/shard_map/ppermute | solution.py:411
  341.2 25.0 %collective-permute-start.17 = (bf16[512,768]{1,0:T(8,128)(2,1)}, bf16[512,768]{1,0:T(8,128)(2,1)}, u32[]{:S(2)}, u32[]{:S(2)}) collective-permute-start(bf16[512,768]{1,0:T(8,128)(2,1)} %get-tuple-element.63), channel_id=1, source_target_pairs={{0,3},{1,2},{4,7},{5,6}} | collective-permute-start | bytes 2359304 | tf_op jit(solution)/shard_map/ppermute | solution.py:411
  343.7 81.3 %collective-permute-start.16 = (bf16[256,6144]{1,0:T(8,128)(2,1)}, bf16[256,6144]{1,0:T(8,128)(2,1)}, u32[]{:S(2)}, u32[]{:S(2)}) collective-permute-start(bf16[256,6144]{1,0:T(8,128)(2,1)} %collective-permute-done.11.refs_1_), channel_id=1, source_target_pairs={{0,2},{1,3},{2,0},{3,1},{4,6},{5,7},{6,4},{7,5}} | collective-permute-start | bytes 9437192 | tf_op jit(solution)/shard_map/ppermute | solution.py:407
  425.0 69.3 %collective-permute-start.18 = (bf16[256,6144]{1,0:T(8,128)(2,1)}, bf16[256,6144]{1,0:T(8,128)(2,1)}, u32[]{:S(2)}, u32[]{:S(2)}) collective-permute-start(bf16[256,6144]{1,0:T(8,128)(2,1)} %collective-permute-done.15.refs_2_), channel_id=1, source_target_pairs={{0,2},{1,3},{2,0},{3,1},{4,6},{5,7},{6,4},{7,5}} | collective-permute-start | bytes 9437192 | tf_op jit(solution)/shard_map/ppermute | solution.py:407
  427.5 121.1 %collective-permute-start.19 = (bf16[256,6144]{1,0:T(8,128)(2,1)S(1)}, bf16[256,6144]{1,0:T(8,128)(2,1)}, u32[]{:S(2)}, u32[]{:S(2)}) collective-permute-start(bf16[256,6144]{1,0:T(8,128)(2,1)S(1)} %copy-done.3), channel_id=1, source_target_pairs={{0,1},{1,0},{2,3},{3,2},{4,5},{5,4},{6,7},{7,6}} | collective-permute-start | bytes 9437192 | tf_op jit(solution)/shard_map/ppermute | solution.py:407
  430.4 116.5 %collective-permute-start.29 = (bf16[256,2304]{1,0:T(8,128)(2,1)}, bf16[256,2304]{1,0:T(8,128)(2,1)}, u32[]{:S(2)}, u32[]{:S(2)}) collective-permute-start(bf16[256,2304]{1,0:T(8,128)(2,1)} %get-tuple-element.46.refs_0_), channel_id=1, source_target_pairs={{0,4},{4,0},{1,5},{5,1},{2,6},{6,2},{3,7},{7,3}} | collective-permute-start | bytes 3538952 | tf_op jit(solution)/shard_map/ppermute | solution.py:415
  433.2 115.5 %collective-permute-start.30 = (bf16[256,768]{1,0:T(8,128)(2,1)S(1)}, bf16[256,768]{1,0:T(8,128)(2,1)}, u32[]{:S(2)}, u32[]{:S(2)}) collective-permute-start(bf16[256,768]{1,0:T(8,128)(2,1)S(1)} %broadcast_select_fusion.3.refs_1_), channel_id=1, source_target_pairs={{0,4},{4,0},{1,5},{5,1},{2,6},{6,2},{3,7},{7,3}} | collective-permute-start | bytes 1179656 | tf_op jit(solution)/shard_map/ppermute | solution.py:415
  435.3 113.9 %collective-permute-start.32 = (bf16[256,768]{1,0:T(8,128)(2,1)}, bf16[256,768]{1,0:T(8,128)(2,1)}, u32[]{:S(2)}, u32[]{:S(2)}) collective-permute-start(bf16[256,768]{1,0:T(8,128)(2,1)} %broadcast_select_fusion.2.refs_3_), channel_id=1, source_target_pairs={{0,4},{4,0},{1,5},{5,1},{2,6},{6,2},{3,7},{7,3}} | collective-permute-start | bytes 1179656 | tf_op jit(solution)/shard_map/ppermute | solution.py:415
  494.3 54.9 %collective-permute-start.31 = (bf16[256,2304]{1,0:T(8,128)(2,1)}, bf16[256,2304]{1,0:T(8,128)(2,1)}, u32[]{:S(2)}, u32[]{:S(2)}) collective-permute-start(bf16[256,2304]{1,0:T(8,128)(2,1)} %get-tuple-element.53.refs_2_), channel_id=1, source_target_pairs={{0,4},{4,0},{1,5},{5,1},{2,6},{6,2},{3,7},{7,3}} | collective-permute-start | bytes 3538952 | tf_op jit(solution)/shard_map/ppermute | solution.py:415
  546.9 12.0 %collective-permute-start.20 = (bf16[256,6144]{1,0:T(8,128)(2,1)}, bf16[256,6144]{1,0:T(8,128)(2,1)}, u32[]{:S(2)}, u32[]{:S(2)}) collective-permute-start(bf16[256,6144]{1,0:T(8,128)(2,1)} %collective-permute-done.11.refs_1_), channel_id=1, source_target_pairs={{0,1},{1,0},{2,3},{3,2},{4,5},{5,4},{6,7},{7,6}} | collective-permute-start | bytes 9437192 | tf_op jit(solution)/shard_map/ppermute | solution.py:407
  548.7 10.0 %collective-permute-start.22 = (bf16[256,6144]{1,0:T(8,128)(2,1)}, bf16[256,6144]{1,0:T(8,128)(2,1)S(1)}, u32[]{:S(2)}, u32[]{:S(2)}) collective-permute-start(bf16[256,6144]{1,0:T(8,128)(2,1)} %collective-permute-done.12.refs_6_), channel_id=1, source_target_pairs={{0,1},{1,0},{2,3},{3,2},{4,5},{5,4},{6,7},{7,6}} | collective-permute-start | bytes 9437192 | tf_op jit(solution)/shard_map/ppermute | solution.py:407
  548.7 14.6 %collective-permute-start.23 = (bf16[256,6144]{1,0:T(8,128)(2,1)}, bf16[256,6144]{1,0:T(8,128)(2,1)}, u32[]{:S(2)}, u32[]{:S(2)}) collective-permute-start(bf16[256,6144]{1,0:T(8,128)(2,1)} %collective-permute-done.16.refs_7_), channel_id=1, source_target_pairs={{0,1},{1,0},{2,3},{3,2},{4,5},{5,4},{6,7},{7,6}} | collective-permute-start | bytes 9437192 | tf_op jit(solution)/shard_map/ppermute | solution.py:407
  549.2 18.6 %collective-permute-start.21 = (bf16[256,6144]{1,0:T(8,128)(2,1)}, bf16[256,6144]{1,0:T(8,128)(2,1)}, u32[]{:S(2)}, u32[]{:S(2)}) collective-permute-start(bf16[256,6144]{1,0:T(8,128)(2,1)} %collective-permute-done.15.refs_2_), channel_id=1, source_target_pairs={{0,1},{1,0},{2,3},{3,2},{4,5},{5,4},{6,7},{7,6}} | collective-permute-start | bytes 9437192 | tf_op jit(solution)/shard_map/ppermute | solution.py:407
  549.2 23.1 %collective-permute-start.24 = (bf16[256,6144]{1,0:T(8,128)(2,1)}, bf16[256,6144]{1,0:T(8,128)(2,1)}, u32[]{:S(2)}, u32[]{:S(2)}) collective-permute-start(bf16[256,6144]{1,0:T(8,128)(2,1)} %collective-permute-done.18.refs_8_), channel_id=1, source_target_pairs={{0,1},{1,0},{2,3},{3,2},{4,5},{5,4},{6,7},{7,6}} | collective-permute-start | bytes 9437192 | tf_op jit(solution)/shard_map/ppermute | solution.py:407
  558.6 42.9 %collective-permute-start.25 = (bf16[256,2304]{1,0:T(8,128)(2,1)}, bf16[256,2304]{1,0:T(8,128)(2,1)}, u32[]{:S(2)}, u32[]{:S(2)}) collective-permute-start(bf16[256,2304]{1,0:T(8,128)(2,1)} %get-tuple-element.59.refs_4_), channel_id=1, source_target_pairs={{0,4},{4,0},{1,5},{5,1},{2,6},{6,2},{3,7},{7,3}} | collective-permute-start | bytes 3538952 | tf_op jit(solution)/shard_map/ppermute | solution.py:415
  558.9 42.7 %collective-permute-start.28 = (bf16[256,768]{1,0:T(8,128)(2,1)}, bf16[256,768]{1,0:T(8,128)(2,1)S(1)}, u32[]{:S(2)}, u32[]{:S(2)}) collective-permute-start(bf16[256,768]{1,0:T(8,128)(2,1)} %broadcast_select_fusion.refs_7_), channel_id=1, source_target_pairs={{0,4},{4,0},{1,5},{5,1},{2,6},{6,2},{3,7},{7,3}} | collective-permute-start | bytes 1179656 | tf_op jit(solution)/shard_map/ppermute | solution.py:415
  563.3 41.4 %collective-permute-start.26 = (bf16[256,768]{1,0:T(8,128)(2,1)}, bf16[256,768]{1,0:T(8,128)(2,1)}, u32[]{:S(2)}, u32[]{:S(2)}) collective-permute-start(bf16[256,768]{1,0:T(8,128)(2,1)} %broadcast_select_fusion.1.refs_5_), channel_id=1, source_target_pairs={{0,4},{4,0},{1,5},{5,1},{2,6},{6,2},{3,7},{7,3}} | collective-permute-start | bytes 1179656 | tf_op jit(solution)/shard_map/ppermute | solution.py:415
  567.8 61.6 %collective-permute-start.27 = (bf16[256,2304]{1,0:T(8,128)(2,1)}, bf16[256,2304]{1,0:T(8,128)(2,1)}, u32[]{:S(2)}, u32[]{:S(2)}) collective-permute-start(bf16[256,2304]{1,0:T(8,128)(2,1)} %get-tuple-element.66.refs_6_), channel_id=1, source_target_pairs={{0,4},{4,0},{1,5},{5,1},{2,6},{6,2},{3,7},{7,3}} | collective-permute-start | bytes 3538952 | tf_op jit(solution)/shard_map/ppermute | solution.py:415
  (12 other events, 354.6 us)

commit v3 on v2

--- a/solution.py
+++ b/solution.py
@@ -55,24 +55,26 @@
 MB = 512
 
 
-def kv_kernel(groups, h_ref, w_ref, b_ref, c_ref, s_ref, k_ref, v_ref, vt_ref, q_ref):
+def kv_kernel(groups, h_ref, w_ref, b_ref, c_ref, s_ref, kv_ref, v_ref, q_ref):
     bias = b_ref[0].astype(F32)
-    first = pl.program_id(0) < groups
-
-    @pl.loop(0, h_ref.shape[0] // MB)
+    i = pl.program_id(0)
+    rows = h_ref.shape[0]
+
+    @pl.loop(0, rows // MB)
     def _(m):
         r = pl.ds(pl.multiple_of(m * MB, MB), MB)
         a = dot(h_ref[r, :], w_ref[...]) + bias
         left = rotate(a[:, :HD], c_ref[r, :], s_ref[r, :]).astype(BF16)
 
-        @pl.when(first)
+        @pl.when(i < groups)
         def _():
-            k_ref[r, :] = left
+            at = pl.multiple_of(jnp.minimum(i, groups - 1) * HD, HD)
+            kv_ref[r, pl.ds(at, HD)] = left
             v = a[:, HD:].astype(BF16)
             v_ref[r, :] = v
-            vt_ref[:, r] = v.T
-
-        @pl.when(jnp.logical_not(first))
+            kv_ref[pl.ds(pl.multiple_of(rows + m * (groups * HD) + at, HD), HD), :] = v.T
+
+        @pl.when(i >= groups)
         def _():
             q_ref[r, :HD] = left
             q_ref[r, HD:] = rotate(a[:, HD:], c_ref[r, :], s_ref[r, :]).astype(BF16)
@@ -81,9 +83,8 @@
 def q_kernel(h_ref, w_ref, b_ref, c_ref, s_ref, q_ref):
     bias = b_ref[0].astype(F32)
 
-    @pl.loop(0, h_ref.shape[0] // MB)
-    def _(m):
-        r = pl.ds(pl.multiple_of(m * MB, MB), MB)
+    for m in range(h_ref.shape[0] // MB):
+        r = pl.ds(m * MB, MB)
         a = dot(h_ref[r, :], w_ref[...]) + bias
         q_ref[r, :HD] = rotate(a[:, :HD], c_ref[r, :], s_ref[r, :]).astype(BF16)
         q_ref[r, HD:] = rotate(a[:, HD:], c_ref[r, :], s_ref[r, :]).astype(BF16)
@@ -101,6 +102,7 @@
 
 
 def project_kv(h, w, b, ce, se, groups):
+    assert groups * HD == MB
     rows, d = h.shape
     per = w.shape[1] // (2 * HD * groups)
     nq = per - 1
@@ -112,15 +114,13 @@
         grid=(steps,),
         in_specs=proj_specs(rows, d, col),
         out_specs=[
+            pl.BlockSpec((2 * rows, MB), lambda i: (0, 0)),
             pl.BlockSpec((rows, HD), lambda i: (0, at(i))),
-            pl.BlockSpec((rows, HD), lambda i: (0, at(i))),
-            pl.BlockSpec((HD, rows), lambda i: (at(i), 0)),
             pl.BlockSpec((rows, 2 * HD), lambda i: (0, jnp.maximum(i - groups, 0))),
         ],
         out_shape=[
+            jax.ShapeDtypeStruct((2 * rows, MB), BF16),
             jax.ShapeDtypeStruct((rows, groups * HD), BF16),
-            jax.ShapeDtypeStruct((rows, groups * HD), BF16),
-            jax.ShapeDtypeStruct((groups * HD, rows), BF16),
             jax.ShapeDtypeStruct((rows, nq * 2 * HD), BF16),
         ],
         compiler_params=pltpu.CompilerParams(vmem_limit_bytes=VLIM),
@@ -147,6 +147,25 @@
     )(h, w, b, ce, se)
 
 
+def cache_kernel(k_ref, v_ref, out_ref):
+    rows, groups, hd = k_ref.shape
+    per = out_ref.shape[1] // rows
+    for g in range(groups):
+        out_ref[:rows, g * hd:(g + 1) * hd] = k_ref[:, g, :]
+        top = rows + g // per * hd
+        out_ref[top:top + hd, g % per * rows:(g % per + 1) * rows] = v_ref[:, g, :].T
+
+
+def pack_cache(k, v):
+    rows, groups, hd = k.shape
+    return pl.pallas_call(
+        cache_kernel,
+        out_shape=jax.ShapeDtypeStruct((2 * rows, groups * hd), BF16),
+        cost_estimate=cost(1e9, 1e6),
+        name="pack_cache",
+    )(k, v)
+
+
 QB = 256
 KB = 1024
 
@@ -154,28 +173,42 @@
 def attn_kernel(chunk, remotes, group, tok, me_ref, q_ref, ql_ref, *refs):
     nr = 1 if remotes else 0
     qr_ref = refs[0] if nr else None
-    kc, vc, ko, vo, ks, vs, kx, vx, kz, vz = refs[nr:nr + 10]
-    outs = refs[nr + 10:nr + 12 + nr]
-    kbuf, vbuf, qt, sbuf, acc, mrun, lrun, obuf, sem = refs[nr + 12 + nr:]
+    pieces = refs[nr:nr + 4]
+    caches = refs[nr + 4:nr + 8]
+    outs = refs[nr + 8:nr + 10 + nr]
+    kbuf, vbuf, qt, sbuf, acc, mrun, lrun, obuf, sem = refs[nr + 10 + nr:]
     g = pl.program_id(0)
     groups = kbuf.shape[0]
     last = groups - 1
     me = me_ref[0]
     mirror = lax.bitwise_xor(me, 3)
-    pieces = [(None, kc, vc), (0, ko, vo), (1, ks, vs), (2, kx, vx), (3, kz, vz)]
+    nc = caches[0].shape[0] // 2
+    ncache = 4 * nc
+    per = caches[0].shape[1] // nc
 
     def each_copy(gg, act):
         reach = jnp.maximum(me, mirror) if gg == last and remotes else me
-        for rel, kp, vp in pieces:
-            n = kp.shape[0]
-            src = None if rel is None else lax.bitwise_xor(me, rel)
-            at = 0 if rel is None else pl.multiple_of(kc.shape[0] + src * tok, tok)
-
-            def go(kp=kp, vp=vp, n=n, at=at):
-                act(pltpu.make_async_copy(kp.at[:, pl.ds(gg * HD, HD)], kbuf.at[gg, pl.ds(at, n), :], sem.at[gg]))
-                act(pltpu.make_async_copy(vp.at[pl.ds(gg * HD, HD), :], vbuf.at[gg, :, pl.ds(at, n)], sem.at[gg]))
-
-            if rel in (None, 0):
+        cols = pl.ds(gg * HD, HD)
+
+        def k_copy(ref, n, at):
+            act(pltpu.make_async_copy(ref.at[pl.ds(0, n), cols], kbuf.at[gg, pl.ds(at, n), :], sem.at[gg]))
+
+        def v_copy(ref, top, left, n, at):
+            act(pltpu.make_async_copy(ref.at[pl.ds(top, HD), pl.ds(left, n)], vbuf.at[gg, :, pl.ds(at, n)], sem.at[gg]))
+
+        for i, ref in enumerate(caches):
+            k_copy(ref, nc, i * nc)
+            v_copy(ref, nc + gg // per * HD, gg % per * nc, nc, i * nc)
+        for rel, ref in enumerate(pieces):
+            src = lax.bitwise_xor(me, rel)
+            at = pl.multiple_of(ncache + src * tok, tok)
+
+            def go(ref=ref, at=at):
+                k_copy(ref, tok, at)
+                for m in range(tok // MB):
+                    v_copy(ref, tok + m * groups * HD + gg * HD, 0, MB, pl.multiple_of(at + m * MB, MB))
+
+            if rel == 0:
                 go()
             else:
                 pl.when(src <= reach)(go)
@@ -202,13 +235,17 @@
     conv = LOG2E * HD ** -0.5
     kvg = jnp.minimum(g, last)
 
-    def step(at, n, mask):
-        k = kbuf[kvg, pl.ds(at, n), :]
+    def keys(at, n):
+        return kbuf[kvg, pl.ds(at, n), :]
+
+    def step(at, n, mask, ahead):
+        k = keys(at, n)
         vt = vbuf[kvg, :, pl.ds(at, n)]
-        sbuf[0, :n] = dot(k, qt[0])
         for h in range(group):
             if h + 1 < group:
                 sbuf[(h + 1) % 2, :n] = dot(k, qt[h + 1])
+            elif ahead is not None:
+                sbuf[(h + 1) % 2] = dot(keys(ahead, KB), qt[0])
             s = sbuf[h % 2, :n]
             if mask is not None:
                 s = jnp.where(mask, s, MASK_VALUE)
@@ -226,17 +263,19 @@
         lrun[...] = jnp.zeros_like(lrun)
         mrun[...] = jnp.full_like(mrun, MASK_VALUE)
 
-        nfull = (kc.shape[0] + jnp.where(g > last, mirror, me) * tok) // KB
+        nfull = (ncache + jnp.where(g > last, mirror, me) * tok) // KB
+
+        sbuf[0] = dot(keys(0, KB), qt[0])
 
         @pl.loop(0, nfull)
         def _(kb):
-            step(pl.multiple_of(kb * KB, KB), KB, None)
+            step(pl.multiple_of(kb * KB, KB), KB, None, pl.multiple_of((kb + 1) * KB, KB))
 
         def finish(c):
             tail = (c + 1) * QB
             key = lax.broadcasted_iota(jnp.int32, (tail, QB), 0)
             row = lax.broadcasted_iota(jnp.int32, (tail, QB), 1)
-            step(pl.multiple_of(nfull * KB, KB), tail, key <= row + c * QB)
+            step(pl.multiple_of(nfull * KB, KB), tail, key <= row + c * QB, None)
 
         others = [(i, c) for i, c in enumerate(remotes) if c != chunk]
         same = g <= last
@@ -263,13 +302,13 @@
             pl.when(g > last)(lambda: put(outs[2]))
 
 
-def attend(chunk, remotes, me, q, ql, qr, pieces, group):
+def attend(chunk, remotes, me, q, ql, qr, pieces, caches, group):
     tok = q.shape[0]
     gw = group * HD
     groups = q.shape[1] // gw + 1
     last = groups - 1
-    ncache = pieces[0].shape[0]
-    total = ncache + 4 * tok
+    total = 2 * caches[0].shape[0] + 4 * tok
+    assert group % 2 == 0 and tok == KB and 2 * caches[0].shape[0] % KB == 0
     anyspec = pl.BlockSpec(memory_space=pl.ANY)
     in_specs = [
         pl.BlockSpec((QB, gw), lambda g, me: (chunk, jnp.minimum(g, last - 1))),
@@ -293,7 +332,7 @@
         grid_spec=pltpu.PrefetchScalarGridSpec(
             num_scalar_prefetch=1,
             grid=(groups + len(remotes),),
-            in_specs=in_specs + [anyspec] * 10,
+            in_specs=in_specs + [anyspec] * 8,
             out_specs=out_specs,
             scratch_shapes=[
                 pltpu.VMEM((groups, total, HD), BF16),
@@ -310,7 +349,7 @@
         out_shape=out_shape,
         compiler_params=pltpu.CompilerParams(vmem_limit_bytes=VLIM),
         cost_estimate=cost(40e9, 12e6),
-    )(me, *args, *pieces)
+    )(me, *args, *pieces, *caches)
 
 
 def gather_rows(pieces, obuf, sem):
@@ -370,19 +409,23 @@
     y_ref, obuf, sem = refs[-3:]
     gather_rows([(r, c, ref) for (r, c), ref in zip(places, pieces)], obuf, sem)
     wr = ws[0].shape[0]
-    total = a_ref[...]
-    for i in range(nw):
-        quarter = lax.bitwise_xor(me, i // nper)
-        at = pl.multiple_of(quarter * (nper * wr) + (i % nper) * wr, wr)
-        total = total + dot(obuf[:, pl.ds(at, wr)], ws[i][...])
-    y_ref[...] = total.astype(BF16)
+
+    @pl.loop(0, obuf.shape[0] // MB)
+    def _(m):
+        r = pl.ds(pl.multiple_of(m * MB, MB), MB)
+        total = a_ref[r, :]
+        for i in range(nw):
+            quarter = lax.bitwise_xor(me, i // nper)
+            at = pl.multiple_of(quarter * (nper * wr) + (i % nper) * wr, wr)
+            total = total + dot(obuf[r, pl.ds(at, wr)], ws[i][...])
+        y_ref[r, :] = total.astype(BF16)
 
 
 def other_part(call, me, chunks, partial, ws, y):
     places = layout(chunks)
     rows = len(chunks) * chunks[0][0].shape[0]
     d = partial.shape[1]
-    nb = 1024
+    nb = 512
     wr = ws[0].shape[0]
     extra = [] if y is None else [y]
     return pl.pallas_call(
@@ -425,7 +468,7 @@
 
 def block(x, k_cache, v_cache, rope_table, norm_gain, w_qkv, b_qkv, w_out):
     tok, d = x.shape
-    ncache, groups, hd = k_cache.shape
+    _, groups, hd = k_cache.shape
     group = w_qkv.shape[1] // (groups * hd) - 2
     cp = lax.axis_index('cp')
     me = cp.astype(jnp.int32).reshape(1)
@@ -436,10 +479,8 @@
     w_parts = [lax.dynamic_slice(w_out, (cp * (nper * wr) + i * wr, 0), (wr, d)) for i in range(nper)]
     wy = [tp_send(p) for p in w_parts]
 
-    cache = jnp.concatenate([k_cache.reshape(ncache, groups * hd), v_cache.reshape(ncache, groups * hd)], axis=1)
-    caches = jnp.concatenate([cache] + [cp_send(cache, r) for r in (1, 2, 3)], axis=0)
-    kc = caches[:, :groups * hd]
-    vc = caches[:, groups * hd:].T
+    cache = pack_cache(k_cache, v_cache)
+    caches = [cache] + [cp_send(cache, r) for r in (1, 2, 3)]
 
     half = rope_table.shape[1] // 2
     spread = jnp.dot(rope_table, spread_matrices(half, hd), precision=lax.Precision.HIGHEST)
@@ -447,14 +488,13 @@
     bias = b_qkv.reshape(-1, 1, 2 * hd)
 
     h = norm(x, norm_gain)
-    k, v, vt, ql = project_kv(h, w_qkv, bias, ce, se, groups)
-    ks, vs = cp_send(k, 1), cp_send(vt, 1)
-    kx, vx = cp_send(k, 2), cp_send(vt, 2)
+    kv, v, ql = project_kv(h, w_qkv, bias, ce, se, groups)
+    kvx = cp_send(kv, 2)
+    kvs = cp_send(kv, 1)
     qr = cp_move(ql, [(2, 1), (3, 0)])
     q = project_q(h, w_qkv, bias, ce, se, groups)
-    (q, kx, vx, wy[0]) = bar((q, kx, vx, wy[0]))
-    kz, vz = cp_send(kx, 1), cp_send(vx, 1)
-    pieces = [kc, vc, k, vt, ks, vs, kx, vx, kz, vz]
+    (q, kvx, wy[0]) = bar((q, kvx, wy[0]))
+    pieces = [kv, kvs, kvx, cp_send(kvx, 1)]
 
     wx, wd, wz = [None] * nper, [None] * nper, [None] * nper
 
@@ -466,7 +506,7 @@
 
     forward(0)
     nchunk = tok // QB
-    remotes = [(0,), (1,), (2, 3), ()]
+    remotes = [(), (0, 1), (2, 3), ()]
     mine, theirs = [], []
     lasts, back, other_last = [None] * nchunk, [None] * nchunk, [None] * nchunk
 
@@ -475,22 +515,22 @@
         other_last[c] = tp_send(lasts[c])
 
     for chunk in range(nchunk):
-        o, lasts[chunk], *rem = attend(chunk, remotes[chunk], me, q, ql, qr, pieces, group)
+        o, lasts[chunk], *rem = attend(chunk, remotes[chunk], me, q, ql, qr, pieces, caches, group)
         if chunk == 0:
-            (o, q) = bar((o, q))
+            (o, q, wy[1]) = bar((o, q, wy[1]))
+            forward(1)
         elif chunk == 1:
-            (o, q, wy[1], wx[0], back[0]) = bar((o, q, wy[1], wx[0], back[0]))
-            forward(1)
+            (o, q, wy[2], wx[0]) = bar((o, q, wy[2], wx[0]))
+            forward(2)
             relay(0)
+        elif chunk == 2:
+            (o, q, back[0], back[1]) = bar((o, q, back[0], back[1]))
             settle(0)
-        elif chunk == 2:
-            (o, q, back[1]) = bar((o, q, back[1]))
             settle(1)
         else:
-            (o, q, wy[2], wx[1], back[2], back[3]) = bar((o, q, wy[2], wx[1], back[2], back[3]))
+            (o, q, wx[1], back[2], back[3]) = bar((o, q, wx[1], back[2], back[3]))
             settle(2)
             settle(3)
-            forward(2)
             relay(1)
         if rem:
             got = cp_move(rem[0], [(0, 3), (1, 2)])
@@ -503,10 +543,8 @@
     (partial, wx[2]) = bar((partial, wx[2]))
     relay(2)
     ws = wy + wd + wx + wz
-    y = None
-    for call in range(nchunk // 2):
-        chunks = [(theirs[c], other_last[c]) for c in (2 * call, 2 * call + 1)]
-        y = other_part(call, me, chunks, partial, ws, y)
+    y = other_part(0, me, list(zip(theirs, other_last)), partial, ws, None)
+    k = kv[:tok]
     return y, k.reshape(tok, groups, hd), v.reshape(tok, groups, hd)
 
 

time: 660 us -> 636 us (0.964)
  starting transfers between devices: 51.1 us -> 35.4 us
  waiting for transfers between devices: 243 us -> 254 us
  other arithmetic: 10.6 us -> 1.66 us
  local copies, waits for them, and re-layouts: 24.5 us -> 17 us
    ppermute x18 -> x15, waiting for transfers between devices: 158 us -> 88.4 us  [cp_send(): return lax.ppermute(v, 'cp', [(i, i ^ rel) for i in range(4)])]
    ppermute x11, waiting for transfers between devices: 84.9 us -> 143 us  [tp_send(): return lax.ppermute(v, 'tp', [(0, 1), (1, 0)])]
    ppermute x4 -> x3, waiting for transfers between devices: 0.01 us -> 22.7 us  [cp_move(): return lax.ppermute(v, 'cp', pairs)]
    ppermute x4 -> x3, starting transfers between devices: 21 us -> 5.39 us  [cp_move(): return lax.ppermute(v, 'cp', pairs)]
    pallas_call x2 -> x1, Pallas kernels: 58.7 us -> 51.1 us  [other_part(): pl.pallas_call(functools.partial(other_kernel, len(ws) // 4, places), gri...]
    ppermute x18 -> x15, starting transfers between devices: 17.2 us -> 17.9 us  [cp_send(): return lax.ppermute(v, 'cp', [(i, i ^ rel) for i in range(4)])]
  transfers between devices with their start and end apart: 33 -> 29, of which waited for: 11 -> 10; matrix products, arithmetic and copies ran while one was open for 5% -> 2% of each run, Pallas kernels for 38% -> 43%
where the time goes in v3:
time: 636 us; the launch traced here: 635 us
  Pallas kernels  325 us (51%)
  waiting for transfers between devices  254 us (40%)
  starting transfers between devices  35.4 us (6%)
  local copies, waits for them, and re-layouts  17 us (3%)
    ppermute x11, waiting for transfers between devices, tp_send(): return lax.ppermute(v, 'tp', [(0, 1), (1, 0)])  143 us
    pallas_call x4, Pallas kernels, attend(): pl.pallas_call(functools.partial(attn_kernel, chunk, remotes, group, tok)...  129 us
    ppermute x15, waiting for transfers between devices, cp_send(): return lax.ppermute(v, 'cp', [(i, i ^ rel) for i in range(4)])  88.4 us
    pallas_call x1, Pallas kernels, other_part(): pl.pallas_call(functools.partial(other_kernel, len(ws) // 4, places), gri...  51.1 us
    pallas_call x1, Pallas kernels, own_part(): pl.pallas_call(functools.partial(own_kernel, places), grid=(d // nb,), in...  50.2 us
    pallas_call x1, Pallas kernels, project_q(): pl.pallas_call(q_kernel, grid=(steps,), in_specs=proj_specs(rows, d, col)...  42 us
    pallas_call x1, Pallas kernels, project_kv(): pl.pallas_call(functools.partial(kv_kernel, groups), grid=(steps,), in_sp...  36.1 us
    ppermute x3, waiting for transfers between devices, cp_move(): return lax.ppermute(v, 'cp', pairs)  22.7 us
  transfers between devices with their start and end apart: 29, of which 10 were waited for; matrix products, arithmetic and copies ran while one was open for 2% of the time, Pallas kernels for 43%

profile of v3, /device:TPU:0, one launch (start us, length us, event | category | flops | bytes accessed | tf_op | source)
XLA Modules:
  0.0 635.3 jit_solution(11420160573133809971)
XLA Ops:
  0.7 7.5 %constant_dynamic-slice_fusion = (bf16[256,6144]{1,0:T(8,128)(2,1)S(1)}, bf16[256,6144]{1,0:T(8,128)(2,1)}, bf16[256,6144]{1,0:T(8,128)(2,1)}) fusion(bf16[3072,6144]{1,0:T(8,128)(2,1)} %w_ref.5, s32[]{:T(128)S(6)} %select_n.32, s32[]{:T(128)S(6)} %select_n.30, s32[]{:T(128)S(6)} %select_n.29), kind=kLoop, calls=%fused_computation.5 | loop fusion | bytes 18874380 | tf_op jit(solution)/shard_map/dynamic_slice | solution.py:479
  8.2 3.3 collective-permute-start.1
  14.8 13.9 %norm.1.h_ref = bf16[1024,6144]{1,0:T(8,128)(2,1)} custom-call(bf16[1024,6144]{1,0:T(8,128)(2,1)} %x_ref.3, bf16[1,6144]{1,0:T(2,128)(2,1)} %reshape.22.g_ref), custom_call_target="tpu_custom_call" | custom-call | flops 503316480 | bytes 25165824 | tf_op jit(solution)/shard_map/norm/pallas_call | solution.py:38
  28.7 36.1 %project_kv.1 = (bf16[2048,512]{1,0:T(8,128)(2,1)}, bf16[1024,512]{1,0:T(8,128)(2,1)}, bf16[1024,768]{1,0:T(8,128)(2,1)}) custom-call(bf16[1024,6144]{1,0:T(8,128)(2,1)} %norm.1.h_ref, bf16[6144,4096]{1,0:T(8,128)(2,1)} %w_ref.4, bf16[16,1,256]{2,1,0:T(2,128)(2,1)} %reshape.26.b_ref, f32[1024,128]{1,0:T(8,128)} %get-tuple-element.73.c_ref, ...), custom_call_target="tpu_custom_call" | custom-call | flops 22548578304 | bytes 34603008 | tf_op jit(solution)/shard_map/project_kv/pallas_call | solution.py:112
  66.3 42.0 %project_q.1.q_ref = bf16[1024,2304]{1,0:T(8,128)(2,1)} custom-call(bf16[1024,6144]{1,0:T(8,128)(2,1)} %norm.1.h_ref, bf16[6144,4096]{1,0:T(8,128)(2,1)} %w_ref.4, bf16[16,1,256]{2,1,0:T(2,128)(2,1)} %reshape.26.b_ref, f32[1024,128]{1,0:T(8,128)} %get-tuple-element.73.c_ref, f32[1024,128]{1,0:T(8,128)} %get-tuple-element.72.s_ref), custom_call_target="tpu_custom_call" | custom-call | flops 28991029248 | bytes 40894464 | tf_op jit(solution)/shard_map/project_q/pallas_call | solution.py:138
  108.3 4.9 collective-permute-done.refs_2_.refs_3_
  113.2 3.2 pack_cache.1.refs_4_.refs_5_
  118.6 12.1 %collective-permute-done.6.refs_7_.refs_8_ = bf16[512,512]{1,0:T(8,128)(2,1)S(1)} collective-permute-done((bf16[512,512]{1,0:T(8,128)(2,1)}, bf16[512,512]{1,0:T(8,128)(2,1)S(1)}, u32[]{:S(2)}, u32[]{:S(2)}) %collective-permute-start.6) | collective-permute-done | bytes 524320 | tf_op jit(solution)/shard_map/ppermute | solution.py:450
  131.2 11.0 %collective-permute-done.5.refs_6_.refs_7_ = bf16[512,512]{1,0:T(8,128)(2,1)} collective-permute-done((bf16[512,512]{1,0:T(8,128)(2,1)}, bf16[512,512]{1,0:T(8,128)(2,1)}, u32[]{:S(2)}, u32[]{:S(2)}) %collective-permute-start.5) | collective-permute-done | bytes 524320 | tf_op jit(solution)/shard_map/ppermute | solution.py:450
  144.1 2.6 collective-permute-start.10
  146.7 18.4 %shard_map.112 = (bf16[256,2304]{1,0:T(8,128)(2,1)}, bf16[256,768]{1,0:T(8,128)(2,1)}) custom-call(s32[1]{0:T(128)} %bitcast.me_ref, bf16[1024,2304]{1,0:T(8,128)(2,1)} %project_q.1.q_ref, bf16[1024,768]{1,0:T(8,128)(2,1)} %get-tuple-element.38.ql_ref, bf16[2048,512]{1,0:T(8,128)(2,1)} %get-tuple-element.36.refs_0_.refs_1_, ...), custom_call_target="tpu_custom_call" | custom-call | flops 40000000000 | bytes 12000000 | tf_op jit(solution)/shard_map/pallas_call | solution.py:330
  165.1 103.8 %collective-permute-done.7.refs_1_ = bf16[256,6144]{1,0:T(8,128)(2,1)} collective-permute-done((bf16[256,6144]{1,0:T(8,128)(2,1)}, bf16[256,6144]{1,0:T(8,128)(2,1)}, u32[]{:S(2)}, u32[]{:S(2)}) %collective-permute-start.7) | collective-permute-done | bytes 3145760 | tf_op jit(solution)/shard_map/ppermute | solution.py:458
  268.9 42.1 %shard_map.113 = (bf16[256,2304]{1,0:T(8,128)(2,1)}, bf16[256,768]{1,0:T(8,128)(2,1)}, bf16[512,768]{1,0:T(8,128)(2,1)}) custom-call(s32[1]{0:T(128)} %bitcast.me_ref, bf16[1024,2304]{1,0:T(8,128)(2,1)} %project_q.1.q_ref, bf16[1024,768]{1,0:T(8,128)(2,1)} %get-tuple-element.38.ql_ref, bf16[1024,768]{1,0:T(8,128)(2,1)} %collective-permute-done.8.refs_0_, ...), custom_call_target="tpu_custom_call" | custom-call | flops 40000000000 | bytes 12000000 | tf_op jit(solution)/shard_map/pallas_call | solution.py:330
  311.0 2.2 collective-permute-start.11
  313.2 4.4 collective-permute-start.15
  317.7 9.2 %collective-permute-done.11 = bf16[512,768]{1,0:T(8,128)(2,1)} collective-permute-done((bf16[512,768]{1,0:T(8,128)(2,1)}, bf16[512,768]{1,0:T(8,128)(2,1)}, u32[]{:S(2)}, u32[]{:S(2)}) %collective-permute-start.11) | collective-permute-done | bytes 786464 | tf_op jit(solution)/shard_map/ppermute | solution.py:454
  326.9 6.2 collective-permute-start.12
  333.1 1.9 fusion.2
  335.0 45.2 %shard_map.114 = (bf16[256,2304]{1,0:T(8,128)(2,1)}, bf16[256,768]{1,0:T(8,128)(2,1)}, bf16[512,768]{1,0:T(8,128)(2,1)}) custom-call(s32[1]{0:T(128)} %bitcast.me_ref, bf16[1024,2304]{1,0:T(8,128)(2,1)} %project_q.1.q_ref, bf16[1024,768]{1,0:T(8,128)(2,1)} %get-tuple-element.38.ql_ref, bf16[1024,768]{1,0:T(8,128)(2,1)} %collective-permute-done.8.refs_0_, ...), custom_call_target="tpu_custom_call" | custom-call | flops 40000000000 | bytes 12000000 | tf_op jit(solution)/shard_map/pallas_call | solution.py:330
  380.2 1.7 collective-permute-start.13
  382.0 23.0 %shard_map.115 = (bf16[256,2304]{1,0:T(8,128)(2,1)}, bf16[256,768]{1,0:T(8,128)(2,1)}) custom-call(s32[1]{0:T(128)} %bitcast.me_ref, bf16[1024,2304]{1,0:T(8,128)(2,1)} %project_q.1.q_ref, bf16[1024,768]{1,0:T(8,128)(2,1)} %get-tuple-element.38.ql_ref, bf16[2048,512]{1,0:T(8,128)(2,1)} %get-tuple-element.36.refs_0_.refs_1_, ...), custom_call_target="tpu_custom_call" | custom-call | flops 40000000000 | bytes 12000000 | tf_op jit(solution)/shard_map/pallas_call | solution.py:330
  405.2 13.5 %collective-permute-done.13 = bf16[512,768]{1,0:T(8,128)(2,1)S(1)} collective-permute-done((bf16[512,768]{1,0:T(8,128)(2,1)}, bf16[512,768]{1,0:T(8,128)(2,1)S(1)}, u32[]{:S(2)}, u32[]{:S(2)}) %collective-permute-start.13) | collective-permute-done | bytes 786464 | tf_op jit(solution)/shard_map/ppermute | solution.py:454
  420.7 1.8 collective-permute-start.22
  422.7 60.3 %collective-permute-done.14.refs_8_ = bf16[256,6144]{1,0:T(8,128)(2,1)} collective-permute-done((bf16[256,6144]{1,0:T(8,128)(2,1)}, bf16[256,6144]{1,0:T(8,128)(2,1)}, u32[]{:S(2)}, u32[]{:S(2)}) %collective-permute-start.14) | collective-permute-done | bytes 3145760 | tf_op jit(solution)/shard_map/ppermute | solution.py:450
  483.4 50.2 %own_part.1.a_ref = f32[1024,6144]{1,0:T(8,128)} custom-call(bf16[1024,6144]{1,0:T(8,128)(2,1)} %x_ref.3, bf16[3072,6144]{1,0:T(8,128)(2,1)} %w_ref.5, bf16[256,2304]{1,0:T(8,128)(2,1)} %get-tuple-element.41.refs_0_, bf16[256,768]{1,0:T(8,128)(2,1)} %copy-done.7, bf16[256,2304]{1,0:T(8,128)(2,1)} %get-tuple-element.50.refs_2_, bf16[256,768]{1,0:T(8,128)(2,1)} %copy-done.9, ...), custom_call_target="tpu_custom_call" | custom-call | flops 38654705664 | bytes 75497472 | tf_op jit(solution)/shard_map/own_part/pallas_call | solution.py:389
  534.6 1.7 collective-permute-start.28
  536.4 9.3 %collective-permute-done.28.refs_19_ = bf16[256,768]{1,0:T(8,128)(2,1)S(1)} collective-permute-done((bf16[256,768]{1,0:T(8,128)(2,1)S(1)}, bf16[256,768]{1,0:T(8,128)(2,1)S(1)}, u32[]{:S(2)}, u32[]{:S(2)}) %collective-permute-start.28) | collective-permute-done | bytes 393248 | tf_op jit(solution)/shard_map/ppermute | solution.py:458
  545.7 1.7 collective-permute-start.26
  547.5 8.5 %collective-permute-done.26.refs_17_ = bf16[256,768]{1,0:T(8,128)(2,1)S(1)} collective-permute-done((bf16[256,768]{1,0:T(8,128)(2,1)S(1)}, bf16[256,768]{1,0:T(8,128)(2,1)S(1)}, u32[]{:S(2)}, u32[]{:S(2)}) %collective-permute-start.26) | collective-permute-done | bytes 393248 | tf_op jit(solution)/shard_map/ppermute | solution.py:458
  556.7 1.7 collective-permute-start.27
  561.9 21.2 %collective-permute-done.27.refs_18_ = bf16[256,2304]{1,0:T(8,128)(2,1)S(1)} collective-permute-done((bf16[256,2304]{1,0:T(8,128)(2,1)}, bf16[256,2304]{1,0:T(8,128)(2,1)S(1)}, u32[]{:S(2)}, u32[]{:S(2)}) %collective-permute-start.27) | collective-permute-done | bytes 1179680 | tf_op jit(solution)/shard_map/ppermute | solution.py:458
  584.1 51.1 %shard_map.116 = bf16[1024,6144]{1,0:T(8,128)(2,1)} custom-call(s32[1]{0:T(128)} %bitcast.me_ref, f32[1024,6144]{1,0:T(8,128)} %own_part.1.a_ref, bf16[256,6144]{1,0:T(8,128)(2,1)} %collective-permute-done.1.refs_0_, bf16[256,6144]{1,0:T(8,128)(2,1)} %collective-permute-done.7.refs_1_, bf16[256,6144]{1,0:T(8,128)(2,1)} %collective-permute-done.9.refs_2_, ...), custom_call_target="tpu_custom_call" | custom-call | flops 38654705664 | bytes 75497472 | tf_op jit(solution)/shard_map/pallas_call | solution.py:431
  (90 shorter events, 18.4 us)
Async XLA Ops:
  8.2 105.0 %collective-permute-start.1 = (bf16[256,6144]{1,0:T(8,128)(2,1)}, bf16[256,6144]{1,0:T(8,128)(2,1)}, u32[]{:S(2)}, u32[]{:S(2)}) collective-permute-start(bf16[256,6144]{1,0:T(8,128)(2,1)} %get-tuple-element.71), channel_id=1, source_target_pairs={{0,4},{4,0},{1,5},{5,1},{2,6},{6,2},{3,7},{7,3}} | collective-permute-start | bytes 9437192 | tf_op jit(solution)/shard_map/ppermute | solution.py:458
  64.8 79.2 %collective-permute-start.2 = (bf16[2048,512]{1,0:T(8,128)(2,1)}, bf16[2048,512]{1,0:T(8,128)(2,1)}, u32[]{:S(2)}, u32[]{:S(2)}) collective-permute-start(bf16[2048,512]{1,0:T(8,128)(2,1)} %get-tuple-element.36.refs_0_.refs_1_), channel_id=1, source_target_pairs={{0,1},{1,0},{2,3},{3,2},{4,5},{5,4},{6,7},{7,6}} | collective-permute-start | bytes 6291464 | tf_op jit(solution)/shard_map/ppermute | solution.py:450
  64.8 48.4 %collective-permute-start = (bf16[2048,512]{1,0:T(8,128)(2,1)}, bf16[2048,512]{1,0:T(8,128)(2,1)}, u32[]{:S(2)}, u32[]{:S(2)}) collective-permute-start(bf16[2048,512]{1,0:T(8,128)(2,1)} %get-tuple-element.36.refs_0_.refs_1_), channel_id=1, source_target_pairs={{0,2},{1,3},{2,0},{3,1},{4,6},{5,7},{6,4},{7,5}} | collective-permute-start | bytes 6291464 | tf_op jit(solution)/shard_map/ppermute | solution.py:450
  113.2 33.5 %collective-permute-start.3 = (bf16[2048,512]{1,0:T(8,128)(2,1)}, bf16[2048,512]{1,0:T(8,128)(2,1)}, u32[]{:S(2)}, u32[]{:S(2)}) collective-permute-start(bf16[2048,512]{1,0:T(8,128)(2,1)} %collective-permute-done.refs_2_.refs_3_), channel_id=1, source_target_pairs={{0,1},{1,0},{2,3},{3,2},{4,5},{5,4},{6,7},{7,6}} | collective-permute-start | bytes 6291464 | tf_op jit(solution)/shard_map/ppermute | solution.py:450
  116.4 14.2 %collective-permute-start.6 = (bf16[512,512]{1,0:T(8,128)(2,1)}, bf16[512,512]{1,0:T(8,128)(2,1)S(1)}, u32[]{:S(2)}, u32[]{:S(2)}) collective-permute-start(bf16[512,512]{1,0:T(8,128)(2,1)} %pack_cache.1.refs_4_.refs_5_), channel_id=1, source_target_pairs={{0,3},{1,2},{2,1},{3,0},{4,7},{5,6},{6,5},{7,4}} | collective-permute-start | bytes 1572872 | tf_op jit(solution)/shard_map/ppermute | solution.py:450
  118.0 24.2 %collective-permute-start.5 = (bf16[512,512]{1,0:T(8,128)(2,1)}, bf16[512,512]{1,0:T(8,128)(2,1)}, u32[]{:S(2)}, u32[]{:S(2)}) collective-permute-start(bf16[512,512]{1,0:T(8,128)(2,1)} %pack_cache.1.refs_4_.refs_5_), channel_id=1, source_target_pairs={{0,2},{1,3},{2,0},{3,1},{4,6},{5,7},{6,4},{7,5}} | collective-permute-start | bytes 1572872 | tf_op jit(solution)/shard_map/ppermute | solution.py:450
  118.6 24.0 %collective-permute-start.4 = (bf16[512,512]{1,0:T(8,128)(2,1)}, bf16[512,512]{1,0:T(8,128)(2,1)}, u32[]{:S(2)}, u32[]{:S(2)}) collective-permute-start(bf16[512,512]{1,0:T(8,128)(2,1)} %pack_cache.1.refs_4_.refs_5_), channel_id=1, source_target_pairs={{0,1},{1,0},{2,3},{3,2},{4,5},{5,4},{6,7},{7,6}} | collective-permute-start | bytes 1572872 | tf_op jit(solution)/shard_map/ppermute | solution.py:450
  130.7 204.3 %collective-permute-start.9 = (bf16[256,6144]{1,0:T(8,128)(2,1)S(1)}, bf16[256,6144]{1,0:T(8,128)(2,1)}, u32[]{:S(2)}, u32[]{:S(2)}) collective-permute-start(bf16[256,6144]{1,0:T(8,128)(2,1)S(1)} %get-tuple-element.69), channel_id=1, source_target_pairs={{0,4},{4,0},{1,5},{5,1},{2,6},{6,2},{3,7},{7,3}} | collective-permute-start | bytes 9437192 | tf_op jit(solution)/shard_map/ppermute | solution.py:458
  142.2 126.7 %collective-permute-start.7 = (bf16[256,6144]{1,0:T(8,128)(2,1)}, bf16[256,6144]{1,0:T(8,128)(2,1)}, u32[]{:S(2)}, u32[]{:S(2)}) collective-permute-start(bf16[256,6144]{1,0:T(8,128)(2,1)} %get-tuple-element.70), channel_id=1, source_target_pairs={{0,4},{4,0},{1,5},{5,1},{2,6},{6,2},{3,7},{7,3}} | collective-permute-start | bytes 9437192 | tf_op jit(solution)/shard_map/ppermute | solution.py:458
  142.6 126.3 %collective-permute-start.8 = (bf16[1024,768]{1,0:T(8,128)(2,1)}, bf16[1024,768]{1,0:T(8,128)(2,1)}, u32[]{:S(2)}, u32[]{:S(2)}) collective-permute-start(bf16[1024,768]{1,0:T(8,128)(2,1)} %get-tuple-element.38.ql_ref), channel_id=1, source_target_pairs={{2,1},{3,0},{6,5},{7,4}} | collective-permute-start | bytes 4718600 | tf_op jit(solution)/shard_map/ppermute | solution.py:454
  144.1 190.9 %collective-permute-start.10 = (bf16[256,6144]{1,0:T(8,128)(2,1)}, bf16[256,6144]{1,0:T(8,128)(2,1)}, u32[]{:S(2)}, u32[]{:S(2)}) collective-permute-start(bf16[256,6144]{1,0:T(8,128)(2,1)} %collective-permute-done.1.refs_0_), channel_id=1, source_target_pairs={{0,2},{1,3},{2,0},{3,1},{4,6},{5,7},{6,4},{7,5}} | collective-permute-start | bytes 9437192 | tf_op jit(solution)/shard_map/ppermute | solution.py:450
  311.0 15.8 %collective-permute-start.11 = (bf16[512,768]{1,0:T(8,128)(2,1)}, bf16[512,768]{1,0:T(8,128)(2,1)}, u32[]{:S(2)}, u32[]{:S(2)}) collective-permute-start(bf16[512,768]{1,0:T(8,128)(2,1)} %get-tuple-element.47), channel_id=1, source_target_pairs={{0,3},{1,2},{4,7},{5,6}} | collective-permute-start | bytes 2359304 | tf_op jit(solution)/shard_map/ppermute | solution.py:454
  313.2 107.4 %collective-permute-start.15 = (bf16[256,6144]{1,0:T(8,128)(2,1)}, bf16[256,6144]{1,0:T(8,128)(2,1)}, u32[]{:S(2)}, u32[]{:S(2)}) collective-permute-start(bf16[256,6144]{1,0:T(8,128)(2,1)} %collective-permute-done.1.refs_0_), channel_id=1, source_target_pairs={{0,1},{1,0},{2,3},{3,2},{4,5},{5,4},{6,7},{7,6}} | collective-permute-start | bytes 9437192 | tf_op jit(solution)/shard_map/ppermute | solution.py:450
  317.6 104.8 %collective-permute-start.21 = (bf16[256,2304]{1,0:T(8,128)(2,1)}, bf16[256,2304]{1,0:T(8,128)(2,1)}, u32[]{:S(2)}, u32[]{:S(2)}) collective-permute-start(bf16[256,2304]{1,0:T(8,128)(2,1)} %get-tuple-element.41.refs_0_), channel_id=1, source_target_pairs={{0,4},{4,0},{1,5},{5,1},{2,6},{6,2},{3,7},{7,3}} | collective-permute-start | bytes 3538952 | tf_op jit(solution)/shard_map/ppermute | solution.py:458
  326.9 91.9 %collective-permute-start.12 = (bf16[256,6144]{1,0:T(8,128)(2,1)}, bf16[256,6144]{1,0:T(8,128)(2,1)}, u32[]{:S(2)}, u32[]{:S(2)}) collective-permute-start(bf16[256,6144]{1,0:T(8,128)(2,1)} %collective-permute-done.7.refs_1_), channel_id=1, source_target_pairs={{0,2},{1,3},{2,0},{3,1},{4,6},{5,7},{6,4},{7,5}} | collective-permute-start | bytes 9437192 | tf_op jit(solution)/shard_map/ppermute | solution.py:450
  380.2 38.5 %collective-permute-start.13 = (bf16[512,768]{1,0:T(8,128)(2,1)}, bf16[512,768]{1,0:T(8,128)(2,1)S(1)}, u32[]{:S(2)}, u32[]{:S(2)}) collective-permute-start(bf16[512,768]{1,0:T(8,128)(2,1)} %get-tuple-element.57), channel_id=1, source_target_pairs={{0,3},{1,2},{4,7},{5,6}} | collective-permute-start | bytes 2359304 | tf_op jit(solution)/shard_map/ppermute | solution.py:454
  381.9 101.1 %collective-permute-start.14 = (bf16[256,6144]{1,0:T(8,128)(2,1)}, bf16[256,6144]{1,0:T(8,128)(2,1)}, u32[]{:S(2)}, u32[]{:S(2)}) collective-permute-start(bf16[256,6144]{1,0:T(8,128)(2,1)} %collective-permute-done.9.refs_2_), channel_id=1, source_target_pairs={{0,2},{1,3},{2,0},{3,1},{4,6},{5,7},{6,4},{7,5}} | collective-permute-start | bytes 9437192 | tf_op jit(solution)/shard_map/ppermute | solution.py:450
  418.7 115.9 %collective-permute-start.16 = (bf16[256,6144]{1,0:T(8,128)(2,1)}, bf16[256,6144]{1,0:T(8,128)(2,1)}, u32[]{:S(2)}, u32[]{:S(2)}) collective-permute-start(bf16[256,6144]{1,0:T(8,128)(2,1)} %collective-permute-done.7.refs_1_), channel_id=1, source_target_pairs={{0,1},{1,0},{2,3},{3,2},{4,5},{5,4},{6,7},{7,6}} | collective-permute-start | bytes 9437192 | tf_op jit(solution)/shard_map/ppermute | solution.py:450
  418.8 114.8 %collective-permute-start.24 = (bf16[256,768]{1,0:T(8,128)(2,1)S(1)}, bf16[256,768]{1,0:T(8,128)(2,1)S(1)}, u32[]{:S(2)}, u32[]{:S(2)}) collective-permute-start(bf16[256,768]{1,0:T(8,128)(2,1)S(1)} %broadcast_select_fusion.2.refs_3_), channel_id=1, source_target_pairs={{0,4},{4,0},{1,5},{5,1},{2,6},{6,2},{3,7},{7,3}} | collective-permute-start | bytes 1179656 | tf_op jit(solution)/shard_map/ppermute | solution.py:458
  420.7 114.0 %copy-start.8 = (bf16[256,768]{1,0:T(8,128)(2,1)S(1)}, bf16[256,768]{1,0:T(8,128)(2,1)}, u32[]{:S(2)}) copy-start(bf16[256,768]{1,0:T(8,128)(2,1)} %broadcast_select_fusion.refs_7_) | copy-start | bytes 1179652
  420.7 125.0 %copy-start.4 = (bf16[256,768]{1,0:T(8,128)(2,1)S(1)}, bf16[256,768]{1,0:T(8,128)(2,1)}, u32[]{:S(2)}) copy-start(bf16[256,768]{1,0:T(8,128)(2,1)} %broadcast_select_fusion.1.refs_5_) | copy-start | bytes 1179652
  420.7 139.0 %copy-start.3 = (bf16[1024,512]{1,0:T(8,128)(2,1)S(1)}, bf16[1024,512]{1,0:T(8,128)(2,1)}, u32[]{:S(2)}) copy-start(bf16[1024,512]{1,0:T(8,128)(2,1)} %get-tuple-element.68) | copy-start | bytes 3145732
  420.7 113.0 %collective-permute-start.22 = (bf16[256,768]{1,0:T(8,128)(2,1)S(1)}, bf16[256,768]{1,0:T(8,128)(2,1)}, u32[]{:S(2)}, u32[]{:S(2)}) collective-permute-start(bf16[256,768]{1,0:T(8,128)(2,1)S(1)} %broadcast_select_fusion.3.refs_1_), channel_id=1, source_target_pairs={{0,4},{4,0},{1,5},{5,1},{2,6},{6,2},{3,7},{7,3}} | collective-permute-start | bytes 1179656 | tf_op jit(solution)/shard_map/ppermute | solution.py:458
  422.4 111.7 %collective-permute-start.25 = (bf16[256,2304]{1,0:T(8,128)(2,1)}, bf16[256,2304]{1,0:T(8,128)(2,1)}, u32[]{:S(2)}, u32[]{:S(2)}) collective-permute-start(bf16[256,2304]{1,0:T(8,128)(2,1)} %get-tuple-element.53.refs_4_), channel_id=1, source_target_pairs={{0,4},{4,0},{1,5},{5,1},{2,6},{6,2},{3,7},{7,3}} | collective-permute-start | bytes 3538952 | tf_op jit(solution)/shard_map/ppermute | solution.py:458
  483.1 51.1 %collective-permute-start.23 = (bf16[256,2304]{1,0:T(8,128)(2,1)}, bf16[256,2304]{1,0:T(8,128)(2,1)}, u32[]{:S(2)}, u32[]{:S(2)}) collective-permute-start(bf16[256,2304]{1,0:T(8,128)(2,1)} %get-tuple-element.50.refs_2_), channel_id=1, source_target_pairs={{0,4},{4,0},{1,5},{5,1},{2,6},{6,2},{3,7},{7,3}} | collective-permute-start | bytes 3538952 | tf_op jit(solution)/shard_map/ppermute | solution.py:458
  533.6 28.3 %collective-permute-start.17 = (bf16[256,6144]{1,0:T(8,128)(2,1)}, bf16[256,6144]{1,0:T(8,128)(2,1)}, u32[]{:S(2)}, u32[]{:S(2)}) collective-permute-start(bf16[256,6144]{1,0:T(8,128)(2,1)} %collective-permute-done.9.refs_2_), channel_id=1, source_target_pairs={{0,1},{1,0},{2,3},{3,2},{4,5},{5,4},{6,7},{7,6}} | collective-permute-start | bytes 9437192 | tf_op jit(solution)/shard_map/ppermute | solution.py:450
  533.6 28.3 %collective-permute-start.18 = (bf16[256,6144]{1,0:T(8,128)(2,1)}, bf16[256,6144]{1,0:T(8,128)(2,1)}, u32[]{:S(2)}, u32[]{:S(2)}) collective-permute-start(bf16[256,6144]{1,0:T(8,128)(2,1)} %collective-permute-done.10.refs_6_), channel_id=1, source_target_pairs={{0,1},{1,0},{2,3},{3,2},{4,5},{5,4},{6,7},{7,6}} | collective-permute-start | bytes 9437192 | tf_op jit(solution)/shard_map/ppermute | solution.py:450
  534.1 48.9 %collective-permute-start.19 = (bf16[256,6144]{1,0:T(8,128)(2,1)}, bf16[256,6144]{1,0:T(8,128)(2,1)}, u32[]{:S(2)}, u32[]{:S(2)}) collective-permute-start(bf16[256,6144]{1,0:T(8,128)(2,1)} %collective-permute-done.12.refs_7_), channel_id=1, source_target_pairs={{0,1},{1,0},{2,3},{3,2},{4,5},{5,4},{6,7},{7,6}} | collective-permute-start | bytes 9437192 | tf_op jit(solution)/shard_map/ppermute | solution.py:450
  534.2 48.9 %collective-permute-start.20 = (bf16[256,6144]{1,0:T(8,128)(2,1)}, bf16[256,6144]{1,0:T(8,128)(2,1)}, u32[]{:S(2)}, u32[]{:S(2)}) collective-permute-start(bf16[256,6144]{1,0:T(8,128)(2,1)} %collective-permute-done.14.refs_8_), channel_id=1, source_target_pairs={{0,1},{1,0},{2,3},{3,2},{4,5},{5,4},{6,7},{7,6}} | collective-permute-start | bytes 9437192 | tf_op jit(solution)/shard_map/ppermute | solution.py:450
  534.6 11.1 %collective-permute-start.28 = (bf16[256,768]{1,0:T(8,128)(2,1)S(1)}, bf16[256,768]{1,0:T(8,128)(2,1)S(1)}, u32[]{:S(2)}, u32[]{:S(2)}) collective-permute-start(bf16[256,768]{1,0:T(8,128)(2,1)S(1)} %copy-done.8), channel_id=1, source_target_pairs={{0,4},{4,0},{1,5},{5,1},{2,6},{6,2},{3,7},{7,3}} | collective-permute-start | bytes 1179656 | tf_op jit(solution)/shard_map/ppermute | solution.py:458
  545.7 10.2 %collective-permute-start.26 = (bf16[256,768]{1,0:T(8,128)(2,1)S(1)}, bf16[256,768]{1,0:T(8,128)(2,1)S(1)}, u32[]{:S(2)}, u32[]{:S(2)}) collective-permute-start(bf16[256,768]{1,0:T(8,128)(2,1)S(1)} %copy-done.4), channel_id=1, source_target_pairs={{0,4},{4,0},{1,5},{5,1},{2,6},{6,2},{3,7},{7,3}} | collective-permute-start | bytes 1179656 | tf_op jit(solution)/shard_map/ppermute | solution.py:458
  556.7 26.4 %collective-permute-start.27 = (bf16[256,2304]{1,0:T(8,128)(2,1)}, bf16[256,2304]{1,0:T(8,128)(2,1)S(1)}, u32[]{:S(2)}, u32[]{:S(2)}) collective-permute-start(bf16[256,2304]{1,0:T(8,128)(2,1)} %get-tuple-element.60.refs_6_), channel_id=1, source_target_pairs={{0,4},{4,0},{1,5},{5,1},{2,6},{6,2},{3,7},{7,3}} | collective-permute-start | bytes 3538952 | tf_op jit(solution)/shard_map/ppermute | solution.py:458
  (17 other events, 399.4 us)
